TPU v7x, 32 devices: a whole 2x2x4 slice. The times are simulated.
32 devices in a mesh: dp: 2 (over x), sw: 4 (over z), sh: 4 (over y, core).
Axes of the slice: x: 2, y: 2, z: 4, core: 2. Of those that a mesh axis runs over, the one named last changes fastest.
Arguments:
- features: bfloat16 [2, 256, 12, 24, 96], P('dp', None, None, 'sh', 'sw'), parts along dimension 0
- latent: bfloat16 [2, 16, 12, 24, 96], P('dp', None, None, 'sh', 'sw'), parts along dimension 0
- gn_gain: float32 [2, 2, 256], replicated
- gn_bias: float32 [2, 2, 256], replicated
- zy_weight: bfloat16 [2, 2, 16, 256], replicated
- zy_bias: float32 [2, 2, 256], replicated
- zb_weight: bfloat16 [2, 2, 16, 256], replicated
- zb_bias: float32 [2, 2, 256], replicated
- conv_weight: bfloat16 [2, 2, 256, 256, 3, 3, 3], replicated
- conv_bias: float32 [2, 2, 256], replicated
- up_weight: bfloat16 [256, 256, 3, 3], replicated
- up_bias: float32 [256], replicated
Outputs:
- output: bfloat16 [2, 256, 12, 48, 192], P('dp', None, None, 'sh', 'sw'), parts along dimension 0
There are 2 independent parts. A program takes and returns all parts, laid end to end along the dimension named above; an argument that names none is the same for every part.
All inputs are finite; a program needn't handle non-finite values.
Results may differ from a plain program's by a relative error of at most 0.013683.
Values are sent between devices in bfloat16 or wider.
A program may use at most 1 GiB of HBM per device.

v0:
```python
import jax
import jax.numpy as jnp
from jax import lax
from jax.sharding import PartitionSpec as P

NUM_GROUPS = 32
GN_EPSILON = 1e-6
CONV_DIMS = ("NCDHW", "OIDHW", "NCDHW")


def solution(mesh):
    n_sh = mesh.shape["sh"]
    n_sw = mesh.shape["sw"]

    def per_channel(values):
        return values[None, :, None, None, None]

    def edge_exchange(values, axis_name, n_dev, dim):
        n_len = values.shape[dim]
        tail = lax.slice_in_dim(values, n_len - 1, n_len, axis=dim)
        head = lax.slice_in_dim(values, 0, 1, axis=dim)
        if n_dev == 1:
            from_prev = jnp.zeros_like(tail)
            from_next = jnp.zeros_like(head)
        else:
            from_prev = lax.ppermute(tail, axis_name, [(i, i + 1) for i in range(n_dev - 1)])
            from_next = lax.ppermute(head, axis_name, [(i + 1, i) for i in range(n_dev - 1)])
        return jnp.concatenate([from_prev, values, from_next], axis=dim)

    def with_border(values):
        return edge_exchange(edge_exchange(values, "sh", n_sh, 3), "sw", n_sw, 4)

    def group_norm(values, gain, shift):
        n_batch, n_chan, n_frame, n_row, n_col = values.shape
        grouped = values.astype(jnp.float32).reshape(n_batch, NUM_GROUPS, n_chan // NUM_GROUPS, n_frame, n_row, n_col)
        local_stats = jnp.stack([jnp.sum(grouped, axis=(2, 3, 4, 5)), jnp.sum(jnp.square(grouped), axis=(2, 3, 4, 5))])
        total_stats = lax.psum(local_stats, ("sh", "sw"))
        count = (n_chan // NUM_GROUPS) * n_frame * n_row * n_col * n_sh * n_sw
        group_mean = total_stats[0] / count
        group_var = jnp.maximum(total_stats[1] / count - jnp.square(group_mean), 0.0)
        inv_std = lax.rsqrt(group_var + GN_EPSILON)
        normed = (grouped - group_mean[:, :, None, None, None, None]) * inv_std[:, :, None, None, None, None]
        return normed.reshape(values.shape) * per_channel(gain) + per_channel(shift)

    def latent_map(latent, weight, bias):
        return jnp.einsum("nzthw,zc->ncthw", latent, weight, preferred_element_type=jnp.float32) + per_channel(bias)

    def causal_conv(bordered, weight, bias):
        first_frame = bordered[:, :, :1]
        padded = jnp.concatenate([first_frame, first_frame, bordered], axis=2)
        conv_out = lax.conv_general_dilated(padded, weight, (1, 1, 1), "VALID", dimension_numbers=CONV_DIMS, preferred_element_type=jnp.float32)
        return (conv_out + per_channel(bias)).astype(jnp.bfloat16)

    def upsample_conv(bordered, weight, bias):
        upsampled = jnp.repeat(jnp.repeat(bordered, 2, axis=3), 2, axis=4)
        n_row = upsampled.shape[3]
        n_col = upsampled.shape[4]
        cropped = upsampled[:, :, :, 1:n_row - 1, 1:n_col - 1]
        conv_out = lax.conv_general_dilated(cropped, weight[:, :, None], (1, 1, 1), "VALID", dimension_numbers=CONV_DIMS, preferred_element_type=jnp.float32)
        return (conv_out + per_channel(bias)).astype(jnp.bfloat16)

    def local_step(features, latent, gn_gain, gn_bias, zy_weight, zy_bias, zb_weight, zb_bias, conv_weight, conv_bias, up_weight, up_bias):
        hidden = features
        for block in range(gn_gain.shape[0]):
            branch = hidden
            for slot in range(2):
                normed = group_norm(branch, gn_gain[block, slot], gn_bias[block, slot])
                mixed = normed * latent_map(latent, zy_weight[block, slot], zy_bias[block, slot]) + latent_map(latent, zb_weight[block, slot], zb_bias[block, slot])
                activated = jax.nn.silu(mixed).astype(jnp.bfloat16)
                branch = causal_conv(with_border(activated), conv_weight[block, slot], conv_bias[block, slot])
            hidden = (hidden.astype(jnp.float32) + branch.astype(jnp.float32)).astype(jnp.bfloat16)
        return upsample_conv(with_border(hidden), up_weight, up_bias)

    data_spec = P("dp", None, None, "sh", "sw")
    return jax.shard_map(local_step, mesh=mesh, in_specs=(data_spec, data_spec) + (P(),) * 10, out_specs=data_spec, check_vma=False)
```

profile of v0, /device:TPU:0, one launch (start us, length us, event | category | flops | bytes accessed | tf_op | source)
XLA Modules:
  0.0 373.0 jit_solution(11305319287143105767)
XLA Ops:
  2.0 35.2 %psum.28 = f32[2,1,32]{2,1,0:T(1,128)S(1)} all-reduce(f32[2,1,32]{2,1,0:T(1,128)S(1)} %pad_maximum_fusion.31), channel_id=1, replica_groups=mesh['dp'=2,'sw'=4,'sh'=4] {'sh','sw'}, use_global_device_ids=true, to_apply=%region_4.5 | all-reduce | flops 64 | bytes 512 | tf_op jit(solution)/shard_map/psum | solution.py:37
  55.5 4.1 %collective-permute-done.3 = bf16[1,256,12,8,1]{1,4,3,2,0:T(2,128)(2,1)S(1)} collective-permute-done((bf16[1,256,12,8,1]{1,4,3,2,0:T(2,128)(2,1)S(1)}, bf16[1,256,12,8,1]{1,4,3,2,0:T(2,128)(2,1)S(1)}, u32[]{:S(2)}, u32[]{:S(2)}) %collective-permute-start.3) | collective-permute-done | bytes 49184 | tf_op jit(solution)/shard_map/ppermute | solution.py:27
  62.1 3.1 reshape.397
  66.0 12.6 %select_reduce_fusion.3 = (f32[256]{0:T(256)S(1)}, f32[256]{0:T(256)S(1)}, f32[12,6,8,4,256]{4,2,3,1,0:T(8,128)}) fusion(pred[8,4]{0,1:T(4,128)(4,1)S(1)} %copy-done.15, f32[256]{0:T(256)S(1)} %bitcast.363, bf16[2,2,256,256,3,3,3]{3,2,6,5,4,1,0:T(8,128)(2,1)} %param.20, bf16[256,14,8,1,7,2]{0,4,5,2,1,3:T(8,128)(2,1)S(1)} %slice.272, ...), kind=kOutput, calls=%fused_computation.63 | convolution fusion | flops 8167292928 | bytes 8539168 | tf_op jit(solution)/shard_map/conv_general_dilated | solution.py:51
  79.1 30.6 %psum.29 = f32[2,1,32]{2,1,0:T(1,128)S(1)} all-reduce(f32[2,1,32]{2,1,0:T(1,128)S(1)} %pad_maximum_fusion.32), channel_id=1, replica_groups=mesh['dp'=2,'sw'=4,'sh'=4] {'sh','sw'}, use_global_device_ids=true, to_apply=%region_9.10 | all-reduce | flops 64 | bytes 512 | tf_op jit(solution)/shard_map/psum | solution.py:37
  114.7 3.2 fusion.120
  120.5 5.6 %collective-permute-done.5 = bf16[1,256,12,1,24]{1,4,3,2,0:T(8,128)(2,1)S(1)} collective-permute-done((bf16[1,256,12,1,24]{1,4,3,2,0:T(8,128)(2,1)S(1)}, bf16[1,256,12,1,24]{1,4,3,2,0:T(8,128)(2,1)S(1)}, u32[]{:S(2)}, u32[]{:S(2)}) %collective-permute-start.5) | collective-permute-done | bytes 147488 | tf_op jit(solution)/shard_map/ppermute | solution.py:27
  126.2 3.4 collective-permute-start.6
  133.3 2.8 collective-permute-done.7
  138.7 3.1 reshape.406
  142.6 11.8 %fusion.100 = f32[12,6,8,4,256]{4,2,3,1,0:T(8,128)S(1)} fusion(bf16[2,2,256,256,3,3,3]{3,2,6,5,4,1,0:T(8,128)(2,1)} %param.20, bf16[256,14,8,1,7,2]{0,4,5,2,1,3:T(8,128)(2,1)S(1)} %slice.278, bf16[256,14,8,1,8,4]{0,4,5,2,1,3:T(8,128)(2,1)S(1)} %copy.30, f32[256]{0:T(256)S(1)} %bitcast.360, pred[8,4]{0,1:T(4,128)(4,1)S(1)} %copy-done.16), kind=kOutput, calls=%fused_computation.107 | convolution fusion | flops 8164343808 | bytes 8537120 | tf_op jit(solution)/shard_map/conv_general_dilated | solution.py:51
  160.0 30.1 %psum.30 = f32[2,1,32]{2,1,0:T(1,128)S(1)} all-reduce(f32[2,1,32]{2,1,0:T(1,128)S(1)} %pad_maximum_fusion.33), channel_id=1, replica_groups=mesh['dp'=2,'sw'=4,'sh'=4] {'sh','sw'}, use_global_device_ids=true, to_apply=%region_14.15 | all-reduce | flops 64 | bytes 512 | tf_op jit(solution)/shard_map/psum | solution.py:37
  195.6 5.7 %collective-permute-done.9 = bf16[1,256,12,1,24]{1,4,3,2,0:T(8,128)(2,1)S(1)} collective-permute-done((bf16[1,256,12,1,24]{1,4,3,2,0:T(8,128)(2,1)S(1)}, bf16[1,256,12,1,24]{1,4,3,2,0:T(8,128)(2,1)S(1)}, u32[]{:S(2)}, u32[]{:S(2)}) %collective-permute-start.9) | collective-permute-done | bytes 147488 | tf_op jit(solution)/shard_map/ppermute | solution.py:27
  201.5 4.1 %collective-permute-start.10 = (bf16[1,256,12,8,1]{1,4,3,2,0:T(2,128)(2,1)S(1)}, bf16[1,256,12,8,1]{1,4,3,2,0:T(2,128)(2,1)S(1)}, u32[]{:S(2)}, u32[]{:S(2)}) collective-permute-start(bf16[1,256,12,8,1]{1,4,3,2,0:T(2,128)(2,1)S(1)} %get-tuple-element.18), channel_id=1, source_target_pairs={{0,4},{4,8},{8,12},{1,5},{5,9},{9,13},{2,6},{6,10},{10,14},{3,7},{... | collective-permute-start | bytes 147464 | tf_op jit(solution)/shard_map/ppermute | solution.py:26
  209.3 2.8 collective-permute-done.11
  214.7 3.1 reshape.411
  218.6 12.6 %select_reduce_fusion.1 = (f32[256]{0:T(256)S(1)}, f32[256]{0:T(256)S(1)}, f32[12,6,8,4,256]{4,2,3,1,0:T(8,128)}) fusion(pred[8,4]{0,1:T(4,128)(4,1)S(1)} %copy-done.16, f32[256]{0:T(256)S(1)} %bitcast.354, bf16[2,2,256,256,3,3,3]{3,2,6,5,4,1,0:T(8,128)(2,1)} %param.20, bf16[256,14,8,1,7,2]{0,4,5,2,1,3:T(8,128)(2,1)S(1)} %slice.284, ...), kind=kOutput, calls=%fused_computation.59 | convolution fusion | flops 8167292928 | bytes 8539168 | tf_op jit(solution)/shard_map/conv_general_dilated | solution.py:51
  231.6 29.8 %psum.31 = f32[2,1,32]{2,1,0:T(1,128)S(1)} all-reduce(f32[2,1,32]{2,1,0:T(1,128)S(1)} %pad_maximum_fusion.34), channel_id=1, replica_groups=mesh['dp'=2,'sw'=4,'sh'=4] {'sh','sw'}, use_global_device_ids=true, to_apply=%region_19.20 | all-reduce | flops 64 | bytes 512 | tf_op jit(solution)/shard_map/psum | solution.py:37
  266.4 3.1 fusion.122
  272.2 5.6 %collective-permute-done.13 = bf16[1,256,12,1,24]{1,4,3,2,0:T(8,128)(2,1)S(1)} collective-permute-done((bf16[1,256,12,1,24]{1,4,3,2,0:T(8,128)(2,1)S(1)}, bf16[1,256,12,1,24]{1,4,3,2,0:T(8,128)(2,1)S(1)}, u32[]{:S(2)}, u32[]{:S(2)}) %collective-permute-start.13) | collective-permute-done | bytes 147488 | tf_op jit(solution)/shard_map/ppermute | solution.py:27
  278.0 4.1 %collective-permute-start.14 = (bf16[1,256,12,8,1]{1,4,3,2,0:T(2,128)(2,1)S(1)}, bf16[1,256,12,8,1]{1,4,3,2,0:T(2,128)(2,1)S(1)}, u32[]{:S(2)}, u32[]{:S(2)}) collective-permute-start(bf16[1,256,12,8,1]{1,4,3,2,0:T(2,128)(2,1)S(1)} %get-tuple-element.16), channel_id=1, source_target_pairs={{0,4},{4,8},{8,12},{1,5},{5,9},{9,13},{2,6},{6,10},{10,14},{3,7},{... | collective-permute-start | bytes 147464 | tf_op jit(solution)/shard_map/ppermute | solution.py:26
  284.4 4.3 %collective-permute-done.15 = bf16[1,256,12,8,1]{1,4,3,2,0:T(2,128)(2,1)S(1)} collective-permute-done((bf16[1,256,12,8,1]{1,4,3,2,0:T(2,128)(2,1)S(1)}, bf16[1,256,12,8,1]{1,4,3,2,0:T(2,128)(2,1)S(1)}, u32[]{:S(2)}, u32[]{:S(2)}) %collective-permute-start.15) | collective-permute-done | bytes 49184 | tf_op jit(solution)/shard_map/ppermute | solution.py:27
  291.3 3.1 reshape.420
  295.1 11.8 %fusion.110 = f32[12,6,8,4,256]{4,2,3,1,0:T(8,128)S(1)} fusion(bf16[2,2,256,256,3,3,3]{3,2,6,5,4,1,0:T(8,128)(2,1)} %param.20, bf16[256,14,8,1,7,2]{0,4,5,2,1,3:T(8,128)(2,1)S(1)} %slice.290, bf16[256,14,8,1,8,4]{0,4,5,2,1,3:T(8,128)(2,1)S(1)} %copy.36, f32[256]{0:T(256)S(1)} %bitcast.349, pred[8,4]{0,1:T(4,128)(4,1)S(1)} %copy-done.17), kind=kOutput, calls=%fused_computation.109 | convolution fusion | flops 8164343808 | bytes 8537120 | tf_op jit(solution)/shard_map/conv_general_dilated | solution.py:51
  311.9 4.2 %collective-permute-start.16 = (bf16[1,256,12,1,24]{1,4,3,2,0:T(8,128)(2,1)S(1)}, bf16[1,256,12,1,24]{1,4,3,2,0:T(8,128)(2,1)S(1)}, u32[]{:S(2)}, u32[]{:S(2)}) collective-permute-start(bf16[1,256,12,1,24]{1,4,3,2,0:T(8,128)(2,1)S(1)} %get-tuple-element.24), channel_id=1, source_target_pairs={{0,1},{1,2},{2,3},{4,5},{5,6},{6,7},{8,9},{9,10},{10,11},{12,13},{... | collective-permute-start | bytes 442376 | tf_op jit(solution)/shard_map/ppermute | solution.py:26
  324.4 4.3 %collective-permute-done.19 = bf16[1,256,12,8,1]{1,4,3,2,0:T(2,128)(2,1)S(1)} collective-permute-done((bf16[1,256,12,8,1]{1,4,3,2,0:T(2,128)(2,1)S(1)}, bf16[1,256,12,8,1]{1,4,3,2,0:T(2,128)(2,1)S(1)}, u32[]{:S(2)}, u32[]{:S(2)}) %collective-permute-start.19) | collective-permute-done | bytes 49184 | tf_op jit(solution)/shard_map/ppermute | solution.py:27
  330.6 3.8 %broadcast_in_dim.10 = bf16[256,12,8,2,26]{0,3,2,4,1:T(2,128)(2,1)} broadcast(bf16[256,12,8,26]{0,2,3,1:T(8,128)(2,1)S(1)} %copy.38), dimensions={0,1,2,4} | broadcast | bytes 3833856 | tf_op jit(solution)/shard_map/broadcast_in_dim | solution.py:55
  334.4 6.5 %broadcast_in_dim.11 = bf16[256,12,16,26]{0,2,3,1:T(8,128)(2,1)} reshape(bf16[256,12,8,2,26]{0,3,2,4,1:T(2,128)(2,1)} %broadcast_in_dim.10) | data formatting | bytes 5111808 | tf_op jit(solution)/shard_map/broadcast_in_dim | solution.py:55
  346.7 10.4 %add_convert_fusion = bf16[12,12,8,7,256]{4,2,3,1,0:T(8,128)(2,1)S(1)} fusion(f32[256]{0:T(256)S(1)} %copy-done.13, pred[8,7]{0,1:T(8,128)(4,1)S(1)} %copy-done.14, bf16[256,12,16,1,7,2]{0,4,5,2,1,3:T(8,128)(2,1)S(1)} %slice.294, bf16[256,12,16,1,8,7]{0,4,5,2,1,3:T(8,128)(2,1)S(1)} %copy.40, bf16[256,256,3,3]{1,0,3,2:T(8,128)(2,1)S(1)} %copy-done), kind=kOutput, calls=%fused_computation.2 | convolution fusion | flops 9540108288 | bytes 12190776 | tf_op jit(solution)/shard_map/conv_general_dilated | solution.py:59
  357.2 4.1 %copy.41 = bf16[12,12,8,7,256]{4,3,2,1,0:T(8,128)(2,1)} copy(bf16[12,12,8,7,256]{4,2,3,1,0:T(8,128)(2,1)S(1)} %add_convert_fusion) | data formatting | bytes 8257536 | tf_op jit(solution)/shard_map/convert_element_type | solution.py:60
  361.3 7.3 %reshape.429 = bf16[12,12,1,56,256]{4,3,1,0,2:T(8,128)(2,1)} reshape(bf16[12,12,8,7,256]{4,3,2,1,0:T(8,128)(2,1)} %copy.41) | data formatting | bytes 8257536 | tf_op jit(solution)/shard_map/convert_element_type | solution.py:60
  368.5 4.0 %slice_bitcast_fusion = bf16[1,256,12,12,48]{1,4,3,2,0:T(8,128)(2,1)} fusion(bf16[12,12,1,56,256]{4,3,1,0,2:T(8,128)(2,1)} %reshape.429), kind=kLoop, calls=%fused_computation.15 | loop fusion | bytes 7077888 | tf_op jit(solution)/shard_map/convert_element_type | solution.py:60
  (166 shorter events, 91.1 us)
Async XLA Ops:
  0.0 346.4 %copy-start = (bf16[256,256,3,3]{1,0,3,2:T(8,128)(2,1)S(1)}, bf16[256,256,3,3]{1,0,3,2:T(8,128)(2,1)}, u32[]{:S(2)}) copy-start(bf16[256,256,3,3]{1,0,3,2:T(8,128)(2,1)} %param.22) | copy-start | bytes 3538948
  0.0 44.5 %copy-start.5 = (bf16[1,256,12,6,24]{1,4,3,2,0:T(8,128)(2,1)S(1)}, bf16[1,256,12,6,24]{1,4,3,2,0:T(8,128)(2,1)}, u32[]{:S(2)}) copy-start(bf16[1,256,12,6,24]{1,4,3,2,0:T(8,128)(2,1)} %param.12) | copy-start | bytes 2654212
  0.0 44.5 %copy-start.1 = (bf16[1,16,12,6,24]{4,1,3,2,0:T(8,128)(2,1)S(1)}, bf16[1,16,12,6,24]{4,1,3,2,0:T(8,128)(2,1)}, u32[]{:S(2)}) copy-start(bf16[1,16,12,6,24]{4,1,3,2,0:T(8,128)(2,1)} %param.13) | copy-start | bytes 165892
  46.2 8.6 %copy-start.6 = (f32[2,2,256]{2,1,0:T(2,128)S(1)}, f32[2,2,256]{2,1,0:T(2,128)}, u32[]{:S(2)}) copy-start(f32[2,2,256]{2,1,0:T(2,128)} %param.21) | copy-start | bytes 12292
  46.3 5.0 %collective-permute-start = (bf16[1,256,12,1,24]{1,4,3,2,0:T(8,128)(2,1)S(1)}, bf16[1,256,12,1,24]{1,4,3,2,0:T(8,128)(2,1)S(1)}, u32[]{:S(2)}, u32[]{:S(2)}) collective-permute-start(bf16[1,256,12,1,24]{1,4,3,2,0:T(8,128)(2,1)S(1)} %get-tuple-element.32), channel_id=1, source_target_pairs={{0,1},{1,2},{2,3},{4,5},{5,6},{6,7},{8,9},{9,10},{10,11},{12,13},{... | collective-permute-start | bytes 442376 | tf_op jit(solution)/shard_map/ppermute | solution.py:26
  47.6 4.0 %collective-permute-start.1 = (bf16[1,256,12,1,24]{1,4,3,2,0:T(8,128)(2,1)S(1)}, bf16[1,256,12,1,24]{1,4,3,2,0:T(8,128)(2,1)S(1)}, u32[]{:S(2)}, u32[]{:S(2)}) collective-permute-start(bf16[1,256,12,1,24]{1,4,3,2,0:T(8,128)(2,1)S(1)} %get-tuple-element.33), channel_id=1, source_target_pairs={{1,0},{2,1},{3,2},{5,4},{6,5},{7,6},{9,8},{10,9},{11,10},{13,12},{... | collective-permute-start | bytes 442376 | tf_op jit(solution)/shard_map/ppermute | solution.py:27
  51.7 3.7 %collective-permute-start.2 = (bf16[1,256,12,8,1]{1,4,3,2,0:T(2,128)(2,1)S(1)}, bf16[1,256,12,8,1]{1,4,3,2,0:T(2,128)(2,1)S(1)}, u32[]{:S(2)}, u32[]{:S(2)}) collective-permute-start(bf16[1,256,12,8,1]{1,4,3,2,0:T(2,128)(2,1)S(1)} %get-tuple-element.22), channel_id=1, source_target_pairs={{0,4},{4,8},{8,12},{1,5},{5,9},{9,13},{2,6},{6,10},{10,14},{3,7},{... | collective-permute-start | bytes 147464 | tf_op jit(solution)/shard_map/ppermute | solution.py:26
  53.0 6.5 %collective-permute-start.3 = (bf16[1,256,12,8,1]{1,4,3,2,0:T(2,128)(2,1)S(1)}, bf16[1,256,12,8,1]{1,4,3,2,0:T(2,128)(2,1)S(1)}, u32[]{:S(2)}, u32[]{:S(2)}) collective-permute-start(bf16[1,256,12,8,1]{1,4,3,2,0:T(2,128)(2,1)S(1)} %get-tuple-element.23), channel_id=1, source_target_pairs={{4,0},{8,4},{12,8},{5,1},{9,5},{13,9},{6,2},{10,6},{14,10},{7,3},{... | collective-permute-start | bytes 147464 | tf_op jit(solution)/shard_map/ppermute | solution.py:27
  114.7 16.3 %copy-start.2 = (bf16[1,16,12,6,24]{4,1,3,2,0:T(8,128)(2,1)S(1)}, bf16[1,16,12,6,24]{4,1,3,2,0:T(8,128)(2,1)}, u32[]{:S(2)}) copy-start(bf16[1,16,12,6,24]{4,1,3,2,0:T(8,128)(2,1)} %param.13) | copy-start | bytes 165892
  117.9 2.6 collective-permute-start.4
  119.2 6.9 %collective-permute-start.5 = (bf16[1,256,12,1,24]{1,4,3,2,0:T(8,128)(2,1)S(1)}, bf16[1,256,12,1,24]{1,4,3,2,0:T(8,128)(2,1)S(1)}, u32[]{:S(2)}, u32[]{:S(2)}) collective-permute-start(bf16[1,256,12,1,24]{1,4,3,2,0:T(8,128)(2,1)S(1)} %get-tuple-element.31), channel_id=1, source_target_pairs={{1,0},{2,1},{3,2},{5,4},{6,5},{7,6},{9,8},{10,9},{11,10},{13,12},{... | collective-permute-start | bytes 442376 | tf_op jit(solution)/shard_map/ppermute | solution.py:27
  126.2 7.1 %collective-permute-start.6 = (bf16[1,256,12,8,1]{1,4,3,2,0:T(2,128)(2,1)S(1)}, bf16[1,256,12,8,1]{1,4,3,2,0:T(2,128)(2,1)S(1)}, u32[]{:S(2)}, u32[]{:S(2)}) collective-permute-start(bf16[1,256,12,8,1]{1,4,3,2,0:T(2,128)(2,1)S(1)} %get-tuple-element.20), channel_id=1, source_target_pairs={{0,4},{4,8},{8,12},{1,5},{5,9},{9,13},{2,6},{6,10},{10,14},{3,7},{... | collective-permute-start | bytes 147464 | tf_op jit(solution)/shard_map/ppermute | solution.py:26
  129.6 6.5 %collective-permute-start.7 = (bf16[1,256,12,8,1]{1,4,3,2,0:T(2,128)(2,1)S(1)}, bf16[1,256,12,8,1]{1,4,3,2,0:T(2,128)(2,1)S(1)}, u32[]{:S(2)}, u32[]{:S(2)}) collective-permute-start(bf16[1,256,12,8,1]{1,4,3,2,0:T(2,128)(2,1)S(1)} %get-tuple-element.21), channel_id=1, source_target_pairs={{4,0},{8,4},{12,8},{5,1},{9,5},{13,9},{6,2},{10,6},{14,10},{7,3},{... | collective-permute-start | bytes 147464 | tf_op jit(solution)/shard_map/ppermute | solution.py:27
  141.9 0.7 copy-start.12
  157.4 33.0 %copy-start.3 = (bf16[1,16,12,6,24]{4,1,3,2,0:T(8,128)(2,1)S(1)}, bf16[1,16,12,6,24]{4,1,3,2,0:T(8,128)(2,1)}, u32[]{:S(2)}) copy-start(bf16[1,16,12,6,24]{4,1,3,2,0:T(8,128)(2,1)} %param.13) | copy-start | bytes 165892
  157.4 33.0 %copy-start.7 = (f32[1,1,256]{2,1,0:T(1,128)S(1)}, f32[1,1,256]{2,1,0:T(1,128)}, u32[]{:S(2)}) copy-start(f32[1,1,256]{2,1,0:T(1,128)} %get-tuple-element.41) | copy-start | bytes 3076
  157.4 33.0 %copy-start.9 = (f32[1,1,256]{2,1,0:T(1,128)S(1)}, f32[1,1,256]{2,1,0:T(1,128)}, u32[]{:S(2)}) copy-start(f32[1,1,256]{2,1,0:T(1,128)} %get-tuple-element.45) | copy-start | bytes 3076
  157.4 33.0 %copy-start.10 = (f32[1,1,256]{2,1,0:T(1,128)S(1)}, f32[1,1,256]{2,1,0:T(1,128)}, u32[]{:S(2)}) copy-start(f32[1,1,256]{2,1,0:T(1,128)} %get-tuple-element.49) | copy-start | bytes 3076
  157.4 33.0 %copy-start.11 = (f32[1,1,256]{2,1,0:T(1,128)S(1)}, f32[1,1,256]{2,1,0:T(1,128)}, u32[]{:S(2)}) copy-start(f32[1,1,256]{2,1,0:T(1,128)} %get-tuple-element.53) | copy-start | bytes 3076
  159.5 33.5 %copy-start.4 = (bf16[1,256,12,6,24]{1,4,3,2,0:T(8,128)(2,1)}, bf16[1,256,12,6,24]{1,4,3,2,0:T(8,128)(2,1)S(1)}, u32[]{:S(2)}) copy-start(bf16[1,256,12,6,24]{1,4,3,2,0:T(8,128)(2,1)S(1)} %get-tuple-element.13) | copy-start | bytes 2654212
  193.0 2.6 collective-permute-start.8
  194.3 7.0 %collective-permute-start.9 = (bf16[1,256,12,1,24]{1,4,3,2,0:T(8,128)(2,1)S(1)}, bf16[1,256,12,1,24]{1,4,3,2,0:T(8,128)(2,1)S(1)}, u32[]{:S(2)}, u32[]{:S(2)}) collective-permute-start(bf16[1,256,12,1,24]{1,4,3,2,0:T(8,128)(2,1)S(1)} %get-tuple-element.29), channel_id=1, source_target_pairs={{1,0},{2,1},{3,2},{5,4},{6,5},{7,6},{9,8},{10,9},{11,10},{13,12},{... | collective-permute-start | bytes 442376 | tf_op jit(solution)/shard_map/ppermute | solution.py:27
  201.5 7.8 %collective-permute-start.10 = (bf16[1,256,12,8,1]{1,4,3,2,0:T(2,128)(2,1)S(1)}, bf16[1,256,12,8,1]{1,4,3,2,0:T(2,128)(2,1)S(1)}, u32[]{:S(2)}, u32[]{:S(2)}) collective-permute-start(bf16[1,256,12,8,1]{1,4,3,2,0:T(2,128)(2,1)S(1)} %get-tuple-element.18), channel_id=1, source_target_pairs={{0,4},{4,8},{8,12},{1,5},{5,9},{9,13},{2,6},{6,10},{10,14},{3,7},{... | collective-permute-start | bytes 147464 | tf_op jit(solution)/shard_map/ppermute | solution.py:26
  205.6 6.5 %collective-permute-start.11 = (bf16[1,256,12,8,1]{1,4,3,2,0:T(2,128)(2,1)S(1)}, bf16[1,256,12,8,1]{1,4,3,2,0:T(2,128)(2,1)S(1)}, u32[]{:S(2)}, u32[]{:S(2)}) collective-permute-start(bf16[1,256,12,8,1]{1,4,3,2,0:T(2,128)(2,1)S(1)} %get-tuple-element.19), channel_id=1, source_target_pairs={{4,0},{8,4},{12,8},{5,1},{9,5},{13,9},{6,2},{10,6},{14,10},{7,3},{... | collective-permute-start | bytes 147464 | tf_op jit(solution)/shard_map/ppermute | solution.py:27
  269.6 2.6 collective-permute-start.12
  270.9 7.0 %collective-permute-start.13 = (bf16[1,256,12,1,24]{1,4,3,2,0:T(8,128)(2,1)S(1)}, bf16[1,256,12,1,24]{1,4,3,2,0:T(8,128)(2,1)S(1)}, u32[]{:S(2)}, u32[]{:S(2)}) collective-permute-start(bf16[1,256,12,1,24]{1,4,3,2,0:T(8,128)(2,1)S(1)} %get-tuple-element.27), channel_id=1, source_target_pairs={{1,0},{2,1},{3,2},{5,4},{6,5},{7,6},{9,8},{10,9},{11,10},{13,12},{... | collective-permute-start | bytes 442376 | tf_op jit(solution)/shard_map/ppermute | solution.py:27
  278.0 6.3 %collective-permute-start.14 = (bf16[1,256,12,8,1]{1,4,3,2,0:T(2,128)(2,1)S(1)}, bf16[1,256,12,8,1]{1,4,3,2,0:T(2,128)(2,1)S(1)}, u32[]{:S(2)}, u32[]{:S(2)}) collective-permute-start(bf16[1,256,12,8,1]{1,4,3,2,0:T(2,128)(2,1)S(1)} %get-tuple-element.16), channel_id=1, source_target_pairs={{0,4},{4,8},{8,12},{1,5},{5,9},{9,13},{2,6},{6,10},{10,14},{3,7},{... | collective-permute-start | bytes 147464 | tf_op jit(solution)/shard_map/ppermute | solution.py:26
  282.2 6.5 %collective-permute-start.15 = (bf16[1,256,12,8,1]{1,4,3,2,0:T(2,128)(2,1)S(1)}, bf16[1,256,12,8,1]{1,4,3,2,0:T(2,128)(2,1)S(1)}, u32[]{:S(2)}, u32[]{:S(2)}) collective-permute-start(bf16[1,256,12,8,1]{1,4,3,2,0:T(2,128)(2,1)S(1)} %get-tuple-element.17), channel_id=1, source_target_pairs={{4,0},{8,4},{12,8},{5,1},{9,5},{13,9},{6,2},{10,6},{14,10},{7,3},{... | collective-permute-start | bytes 147464 | tf_op jit(solution)/shard_map/ppermute | solution.py:27
  311.9 5.5 %collective-permute-start.16 = (bf16[1,256,12,1,24]{1,4,3,2,0:T(8,128)(2,1)S(1)}, bf16[1,256,12,1,24]{1,4,3,2,0:T(8,128)(2,1)S(1)}, u32[]{:S(2)}, u32[]{:S(2)}) collective-permute-start(bf16[1,256,12,1,24]{1,4,3,2,0:T(8,128)(2,1)S(1)} %get-tuple-element.24), channel_id=1, source_target_pairs={{0,1},{1,2},{2,3},{4,5},{5,6},{6,7},{8,9},{9,10},{10,11},{12,13},{... | collective-permute-start | bytes 442376 | tf_op jit(solution)/shard_map/ppermute | solution.py:26
  316.1 4.0 %collective-permute-start.17 = (bf16[1,256,12,1,24]{1,4,3,2,0:T(8,128)(2,1)S(1)}, bf16[1,256,12,1,24]{1,4,3,2,0:T(8,128)(2,1)S(1)}, u32[]{:S(2)}, u32[]{:S(2)}) collective-permute-start(bf16[1,256,12,1,24]{1,4,3,2,0:T(8,128)(2,1)S(1)} %get-tuple-element.25), channel_id=1, source_target_pairs={{1,0},{2,1},{3,2},{5,4},{6,5},{7,6},{9,8},{10,9},{11,10},{13,12},{... | collective-permute-start | bytes 442376 | tf_op jit(solution)/shard_map/ppermute | solution.py:27
  320.3 4.1 %collective-permute-start.18 = (bf16[1,256,12,8,1]{1,4,3,2,0:T(2,128)(2,1)S(1)}, bf16[1,256,12,8,1]{1,4,3,2,0:T(2,128)(2,1)S(1)}, u32[]{:S(2)}, u32[]{:S(2)}) collective-permute-start(bf16[1,256,12,8,1]{1,4,3,2,0:T(2,128)(2,1)S(1)} %get-tuple-element.14), channel_id=1, source_target_pairs={{0,4},{4,8},{8,12},{1,5},{5,9},{9,13},{2,6},{6,10},{10,14},{3,7},{... | collective-permute-start | bytes 147464 | tf_op jit(solution)/shard_map/ppermute | solution.py:26
  322.2 6.5 %collective-permute-start.19 = (bf16[1,256,12,8,1]{1,4,3,2,0:T(2,128)(2,1)S(1)}, bf16[1,256,12,8,1]{1,4,3,2,0:T(2,128)(2,1)S(1)}, u32[]{:S(2)}, u32[]{:S(2)}) collective-permute-start(bf16[1,256,12,8,1]{1,4,3,2,0:T(2,128)(2,1)S(1)} %get-tuple-element.15), channel_id=1, source_target_pairs={{4,0},{8,4},{12,8},{5,1},{9,5},{13,9},{6,2},{10,6},{14,10},{7,3},{... | collective-permute-start | bytes 147464 | tf_op jit(solution)/shard_map/ppermute | solution.py:27
  (6 other events, 4.3 us)
where the time goes:
time: 379 us; the launch traced here: 373 us
  blocking collectives  126 us (33%)
  matrix products  78.4 us (21%)
  local copies, waits for them, and re-layouts  76.8 us (20%)
  waiting for transfers between devices  39.9 us (11%)
  starting transfers between devices  37.9 us (10%)
  other arithmetic  13 us (3%)
    psum x4, blocking collectives, group_norm(): total_stats = lax.psum(local_stats, ('sh', 'sw'))  126 us
    conv_general_dilated x4, matrix products, causal_conv(): lax.conv_general_dilated(padded, weight, (1, 1, 1), 'VALID', dimension_nu...  48.8 us
    ppermute x10, waiting for transfers between devices, edge_exchange(): lax.ppermute(head, axis_name, [(i + 1, i) for i in range(n_dev - 1)])  38.3 us
    ppermute x10, starting transfers between devices, edge_exchange(): lax.ppermute(tail, axis_name, [(i, i + 1) for i in range(n_dev - 1)])  24.2 us
    dot_general x8, matrix products, latent_map(): jnp.einsum('nzthw,zc->ncthw', latent, weight, preferred_element_type=jnp....  19.1 us
    convert_element_type x3, local copies, waits for them, and re-layouts, upsample_conv(): return (conv_out + per_channel(bias)).astype(jnp.bfloat16)  15.4 us
    conv_general_dilated x12, local copies, waits for them, and re-layouts, causal_conv(): lax.conv_general_dilated(padded, weight, (1, 1, 1), 'VALID', dimension_nu...  15.3 us
    ppermute x10, starting transfers between devices, edge_exchange(): lax.ppermute(head, axis_name, [(i + 1, i) for i in range(n_dev - 1)])  13.7 us
  transfers between devices with their start and end apart: 20, of which 12 were waited for; matrix products, arithmetic and copies ran while one was open for 2% of the time, Pallas kernels for 0%

commit v1 on v0

v1 whole, which is shorter than its diff:
```python
import functools

import jax
import jax.numpy as jnp
from jax import lax
from jax.experimental import pallas as pl
from jax.experimental.pallas import tpu as pltpu
from jax.sharding import PartitionSpec as P

GN_EPSILON = 1e-6
MESH = pl.DeviceIdType.MESH
F32 = jnp.float32
CONTRACT_LAST = (((1,), (1,)), ((), ()))
BF16 = jnp.bfloat16
T, H, W, C, LZ = 12, 6, 24, 256, 16
HE = H + 2
FR = T * W
NA, NB = T * 16, T * 8
AR = (T + 2) * 16 + (T // 2 + 2) * 16
ABASE = (T + 2) * 16
SW_ = 40
T2 = T // 2


LN = 128
PAIR = range(2)
TR = 16


def lanes(half):
    return pl.ds(half * LN, LN)


def tile(i):
    return pl.ds(i * TR, TR)


def chan(ref, b, s):
    return ref[b, pl.ds(s, 1), :]


def acc_specs():
    specs = []
    for q in PAIR:
        for _ in range(3):
            specs += [pltpu.ACC(q)((NA, C), F32), pltpu.ACC(q)((NB, C), F32)]
    return specs


def write_operand(a_ref, s_ref, h):
    for half in PAIR:
        ln = lanes(half)
        for kw in range(3):
            tails = []
            for t in range(T):
                body = s_ref[half, pl.ds(t * SW_ + 7 + kw, 16), :].astype(BF16)
                a_ref[kw, h, tile(t + 2), ln] = body
                if t == 0:
                    a_ref[kw, h, tile(0), ln] = body
                    a_ref[kw, h, tile(1), ln] = body
                tails.append(s_ref[half, pl.ds(t * SW_ + 23 + kw, 8), :])
            pairs = [(max(t, 0), t + T2) for t in range(-2, T2)]
            for i, (p, n) in enumerate(pairs):
                both = jnp.concatenate([tails[p], tails[n]], axis=0).astype(BF16)
                a_ref[kw, h, pl.ds(ABASE + i * TR, TR), ln] = both


def stage_kernel(n_sh, n_sw, feat, lat, gain, gbias, zyw, zyb, zbw, zbb, cw, cb,
                 xe_out, ce_out,
                 wv, a_ref, rx, xres, cv, yv, bv, lt, ltf, lv, fb, re, ce, rs, cs, lts, sv, wz,
                 stat_out, stat_in, par,
                 ld_sem, w_sem, hs_sem, hr_sem, ls_sem, lr_sem, ss_sem, sr_sem):
    n_dev = n_sh * n_sw
    sh = lax.axis_index("sh")
    sw = lax.axis_index("sw")
    me = sh * n_sw + sw
    has = {"u": sh > 0, "d": sh < n_sh - 1, "l": sw > 0, "r": sw < n_sw - 1}

    ld_feat = pltpu.make_async_copy(feat, fb, ld_sem.at[0])
    ld_lat = pltpu.make_async_copy(lat, lv, ld_sem.at[1])
    ld_feat.start()
    ld_lat.start()

    def ld_weight(n, b, s):
        return pltpu.make_async_copy(cw.at[b, s], wv.at[n], w_sem.at[n])

    for n in range(4):
        ld_weight(n, n // 2, n % 2).start()

    zero_rows = jnp.zeros((FR, 128), BF16)
    for i in (0, HE - 1, HE):
        lt[i] = zero_rows

    def peer_of(j):
        p = lax.rem(me + j, n_dev)
        return p, {"sh": p // n_sw, "sw": lax.rem(p, n_sw)}

    bar = pltpu.get_barrier_semaphore()
    for j in range(1, n_dev):
        pl.semaphore_signal(bar, inc=1, device_id=peer_of(j)[1], device_id_type=MESH)

    dirs = [(-1, 0), (1, 0), (0, -1), (0, 1), (-1, -1), (-1, 1), (1, -1), (1, 1)]

    def exists(dy, dx):
        c = None
        for cond, use in ((has["u"], dy < 0), (has["d"], dy > 0), (has["l"], dx < 0), (has["r"], dx > 0)):
            if use:
                c = cond if c is None else jnp.logical_and(c, cond)
        return c

    def device(dy, dx):
        return {"sh": sh + dy, "sw": sw + dx}

    def halo_refs(e, dy, dx, src0):
        side = 1 if dx < 0 else 0
        row = HE - 1 if dy < 0 else 0
        if dx == 0:
            src = (src0[0] if dy < 0 else src0[1])
            return src, re.at[e, 1 if dy < 0 else 0]
        col = 0 if dx < 0 else 1
        if dy == 0:
            return cs.at[col], ce.at[e, side, pl.ds(1, H)]
        return cs.at[col, 0 if dy < 0 else H - 1], ce.at[e, side, row]

    def halo_copy(e, d, src0):
        dy, dx = dirs[d]
        src, dst = halo_refs(e, dy, dx, src0)
        return pltpu.make_async_remote_copy(src_ref=src, dst_ref=dst, send_sem=hs_sem.at[e, d],
                                            recv_sem=hr_sem.at[e, d], device_id=device(dy, dx), device_id_type=MESH)

    def lat_copy(d):
        dy, dx = dirs[d]
        if dx == 0:
            src, dst = (lt.at[1], lt.at[HE - 1]) if dy < 0 else (lt.at[H], lt.at[0])
        else:
            col = 0 if dx < 0 else 1
            base = 128 if dx < 0 else 0
            if dy == 0:
                src, dst = lts.at[col], lt.at[HE, pl.ds(base + 16, H * 16)]
            else:
                row = 0 if dy < 0 else H - 1
                there = (HE - 1 if dy < 0 else 0) * 16
                src, dst = lts.at[col, tile(row)], lt.at[HE, pl.ds(base + there, 16)]
        return pltpu.make_async_remote_copy(src_ref=src, dst_ref=dst, send_sem=ls_sem.at[d],
                                            recv_sem=lr_sem.at[d], device_id=device(dy, dx), device_id_type=MESH)

    def for_dirs(make, what):
        for d, (dy, dx) in enumerate(dirs):
            if what == "recv":
                @pl.when(exists(-dy, -dx))
                def _(d=d):
                    make(d).wait_recv()
            else:
                @pl.when(exists(dy, dx))
                def _(d=d):
                    if what == "start":
                        make(d).start()
                    else:
                        make(d).wait_send()

    def stat_copy(n, j):
        p, dev = peer_of(j)
        return pltpu.make_async_remote_copy(src_ref=stat_out.at[n], dst_ref=stat_in.at[n, me], send_sem=ss_sem.at[n, j],
                                            recv_sem=sr_sem.at[n, me], device_id=dev, device_id_type=MESH)

    def send_stats(n, pivot, s1, s2):
        count = float(T * H * W)
        s1 = jnp.sum(s1, axis=0, keepdims=True) * (1.0 / count)
        s2 = jnp.sum(s2, axis=0, keepdims=True) * (1.0 / count)
        mean = pivot + s1
        var = jnp.maximum(s2 - s1 * s1, 0.0)
        rows = [mean[:, :128], mean[:, 128:], var[:, :128], var[:, 128:]]
        packed = jnp.concatenate(rows + [jnp.zeros((4, 128), F32)], axis=0)
        stat_out[n] = packed
        stat_in[n, me] = packed
        for j in range(1, n_dev):
            stat_copy(n, j).start()

    def recv_stats(n, b, s):
        for j in range(1, n_dev):
            p = lax.rem(me + j, n_dev)
            pltpu.make_async_remote_copy(src_ref=stat_out.at[n], dst_ref=stat_in.at[n, p], send_sem=ss_sem.at[n, j],
                                         recv_sem=sr_sem.at[n, p], device_id=peer_of(j)[1], device_id_type=MESH).wait_recv()
        vals = [stat_in[n, i] for i in range(n_dev)]
        total = functools.reduce(jnp.add, vals) * (1.0 / n_dev)
        mean = total[0:2, :]
        dev = functools.reduce(jnp.add, [jnp.square(v[0:2, :] - mean) for v in vals]) * (1.0 / n_dev)
        var = total[2:4, :] + dev
        lane = lax.broadcasted_iota(jnp.int32, (2, 128), 1)
        for gap in (1, 2, 4):
            low = (lane & gap) == 0

            def partner(v):
                return jnp.where(low, pltpu.roll(v, LN - gap, 1), pltpu.roll(v, gap, 1))

            mp, vp = partner(mean), partner(var)
            half_gap = (mean - mp) * 0.5
            var = (var + vp) * 0.5 + half_gap * half_gap
            mean = (mean + mp) * 0.5
        rstd = lax.rsqrt(var + GN_EPSILON)
        mean = jnp.concatenate([mean[0:1], mean[1:2]], axis=1)
        rstd = jnp.concatenate([rstd[0:1], rstd[1:2]], axis=1)
        par[0] = jnp.broadcast_to(mean, (8, C))
        par[1] = jnp.broadcast_to(rstd * chan(gain, b, s), (8, C))
        par[2] = jnp.broadcast_to(chan(gbias, b, s), (8, C))

    def fill_columns():
        for h in range(H):
            for side, w in ((0, 0), (1, W - 1)):
                for half in PAIR:
                    v = rx[half, pl.ds((h + 1) * FR + w, 16, stride=W), :]
                    cs[side, h, :, lanes(half)] = v.astype(BF16)

    def main():
        ld_feat.wait()
        pivot0 = fb[0, 0, pl.ds(0, 8), :].astype(F32)[0:1, :]
        pivot8 = jnp.broadcast_to(pivot0, (8, C))

        def load_row(h, carry):
            s1, s2 = carry
            for t in range(T):
                x = fb[t, h].astype(F32)
                for half in PAIR:
                    rx[half, pl.ds((h + 1) * FR + t * W, W), :] = x[:, half * LN:half * LN + LN]
                xres[h, pl.ds(t * W, W), :] = x
                for i in range(3):
                    d = x[i * 8:i * 8 + 8] - pivot8
                    s1 = s1 + d
                    s2 = s2 + d * d
            return s1, s2

        zero8 = jnp.zeros((8, C), F32)
        s1, s2 = lax.fori_loop(0, H, load_row, (zero8, zero8))
        for t in range(T):
            rs[0, t] = fb[t, 0]
            rs[1, t] = fb[t, H - 1]
        fill_columns()
        pl.semaphore_wait(bar, n_dev - 1)
        send_stats(0, pivot0, s1, s2)
        row_src = (rs.at[0], rs.at[1])
        for_dirs(lambda d: halo_copy(0, d, row_src), "start")

        ltf[...] = jnp.zeros(ltf.shape, F32)
        ld_lat.wait()

        def turn_row(h, c):
            for t in range(T):
                ltf[pl.ds(h * FR + t * W, W), pl.ds(0, LZ)] = lv[t, h].astype(F32).T
            row = ltf[pl.ds(pl.multiple_of(h * FR, 16), FR), :].astype(BF16)
            lt[h + 1] = row
            return c

        lax.fori_loop(0, H, turn_row, 0)
        for h in range(H):
            for side, w in ((0, 0), (1, W - 1)):
                lts[side, tile(h), :] = ltf[pl.ds(h * FR + w, 16, stride=W), :].astype(BF16)
        for_dirs(lat_copy, "start")
        wz[...] = jnp.zeros(wz.shape, BF16)
        for_dirs(lat_copy, "recv")
        for_dirs(lat_copy, "send")

        half_or_zero = {k: jnp.where(v, 0.5, 0.0).astype(F32) for k, v in has.items()}

        def latent_maps(b, s):
            wz[pl.ds(0, LZ), pl.ds(0, C)] = zyw[b, s]
            wz[pl.ds(0, LZ), pl.ds(C, C)] = zbw[b, s]
            biases = (chan(zyb, b, s), chan(zbb, b, s))
            for i in range(HE + 1):
                v = jnp.dot(lt[i], wz[...], preferred_element_type=F32)
                for q, out in ((0, yv), (1, bv)):
                    m = v[:, q * C:q * C + C] + biases[q]
                    if i < HE:
                        f = half_or_zero["u"] if i == 0 else half_or_zero["d"] if i == HE - 1 else 0.5
                        out[i] = m * f
                    else:
                        for seg in range(2 * HE):
                            f = half_or_zero["l" if seg < HE else "r"]
                            if seg % HE == 0:
                                f = f * half_or_zero["u"] * 2.0
                            if seg % HE == HE - 1:
                                f = f * half_or_zero["d"] * 2.0
                            out[i, tile(seg), :] = m[seg * TR:seg * TR + TR] * f

        def activate(x, y, b):
            n = x.shape[0] // 8
            x, y, b = (v.reshape(n, 8, C) for v in (x, y, b))
            hv = ((x - par[0][None]) * par[1][None] + par[2][None]) * y + b
            return (hv * jnp.tanh(hv) + hv).reshape(n * 8, C)

        def halo_rows(e):
            for i, cond in ((0, has["u"]), (1, has["d"])):
                row = 0 if i == 0 else HE - 1
                for t in range(T):
                    v = jnp.where(cond, re[e, i, t].astype(F32), 0.0)
                    for half in PAIR:
                        rx[half, pl.ds(row * FR + t * W, W), :] = v[:, half * LN:half * LN + LN]

        def col_vals(e, side, h):
            cond = has["l"] if side == 0 else has["r"]
            cond = jnp.logical_and(cond, jnp.logical_or(h > 0, has["u"]))
            cond = jnp.logical_and(cond, jnp.logical_or(h < HE - 1, has["d"]))
            return jnp.where(cond, ce[e, side, h].astype(F32), 0.0)

        def activate_rows(n):
            def row(h, c):
                for side in PAIR:
                    k = side * 128 + h * 16
                    v = activate(col_vals(n, side, h), yv[HE, pl.ds(pl.multiple_of(k, TR), TR), :], bv[HE, pl.ds(pl.multiple_of(k, TR), TR), :])
                    for half in PAIR:
                        sv[half, pl.ds(7 + side * 25, T, stride=SW_), :] = v[0:T, half * LN:half * LN + LN]
                for t in range(T):
                    x = jnp.concatenate([rx[half, pl.ds(pl.multiple_of(h * FR, 8) + t * W, W), :] for half in PAIR], axis=1)
                    v = activate(x, yv[h, pl.ds(t * W, W), :], bv[h, pl.ds(t * W, W), :])
                    for half in PAIR:
                        sv[half, pl.ds(t * SW_ + 8, W), :] = v[:, half * LN:half * LN + LN]
                write_operand(a_ref, sv, h)
                return c

            lax.fori_loop(0, HE, row, 0)

        def conv(n):
            def lhs(h, part, tap):
                kt, kh, kw = tap // 9, tap // 3 % 3, tap % 3
                return a_ref[kw, h + kh, pl.ds(kt * 16 + (ABASE if part else 0), NB if part else NA), :]

            for i in range(9):
                rhs = jnp.concatenate([wv[n, i * 3 + kw] for kw in range(3)], axis=1)
                for h in range(H):
                    cols = [jnp.concatenate([lhs(h, part, i * 3 + kw) for part in PAIR], axis=0) for kw in range(3)]
                    v = lax.dot_general(jnp.concatenate(cols, axis=1), rhs, CONTRACT_LAST, preferred_element_type=F32)
                    if i == 0:
                        cv[h] = v
                    else:
                        cv[h] += v

        def finish(b, s):
            bias = chan(cb, b, s)
            pivot = None
            s1 = s2 = zero8
            for hh in range(3):
                for q in PAIR:
                    h = q * 3 + hh
                    for part in PAIR:
                        v = (cv[h, pl.ds(NA if part else 0, NB if part else NA), :] + bias).astype(BF16).astype(F32)
                        nblk = 16 if part == 0 else 8
                        for i in range(T):
                            if part == 0:
                                t, w0 = i, 0
                            else:
                                t, w0 = (i // 2) + (i % 2) * T2, 16
                            blk = v[i * nblk:(i + 1) * nblk]
                            r0 = t * W + w0
                            if s == 1:
                                blk = (blk + xres[h, pl.ds(r0, nblk), :]).astype(BF16).astype(F32)
                                xres[h, pl.ds(r0, nblk), :] = blk
                            for half in PAIR:
                                rx[half, pl.ds((h + 1) * FR + r0, nblk), :] = blk[:, half * LN:half * LN + LN]
                            if h in (0, H - 1):
                                rs[0 if h == 0 else 1, t, pl.ds(w0, nblk), :] = blk.astype(BF16)
                            if s == 1:
                                xe_out[h + 1, t, pl.ds(w0, nblk), :] = blk.astype(BF16)
                            if pivot is None:
                                pivot = blk[0:1, :]
                            for k in range(nblk // 8):
                                d = blk[k * 8:k * 8 + 8] - pivot
                                s1 = s1 + d
                                s2 = s2 + d * d
            return pivot, s1, s2

        def block(b, carry):
            for s in PAIR:
                n = b * 2 + s
                latent_maps(b, s)
                for_dirs(lambda d: halo_copy(n, d, row_src), "recv")
                halo_rows(n)
                recv_stats(n, b, s)
                activate_rows(n)
                ld_weight(n, b, s).wait()
                conv(n)
                for_dirs(lambda d: halo_copy(n, d, row_src), "send")
                pivot, s1, s2 = finish(b, s)
                if s == 0:
                    send_stats(n + 1, pivot, s1, s2)
                else:
                    @pl.when(b == 0)
                    def _():
                        send_stats(n + 1, pivot, s1, s2)
                fill_columns()
                for_dirs(lambda d: halo_copy(n + 1, d, row_src), "start")
            return carry

        lax.fori_loop(0, 2, block, 0)

        for_dirs(lambda d: halo_copy(4, d, row_src), "recv")
        for i, cond in ((0, has["u"]), (1, has["d"])):
            row = 0 if i == 0 else HE - 1
            for t in range(T):
                xe_out[row, t] = jnp.where(cond, re[4, i, t].astype(F32), 0.0).astype(BF16)
        for side in PAIR:
            for h in range(HE):
                ce_out[side, h] = col_vals(4, side, h).astype(BF16)
        for_dirs(lambda d: halo_copy(4, d, row_src), "send")
        for n in range(4):
            for j in range(1, n_dev):
                stat_copy(n, j).wait_send()

    main()


def up_kernel(xe, ce, wu, ub, out, a_ref, sv, o32, ob, o_sem):
    def row(h, c):
        for side in PAIR:
            v = ce[side, h].astype(F32)
            for half in PAIR:
                sv[half, pl.ds(7 + side * 25, T, stride=SW_), :] = v[0:T, half * LN:half * LN + LN]
        for t in range(T):
            v = xe[h, t].astype(F32)
            for half in PAIR:
                sv[half, pl.ds(t * SW_ + 8, W), :] = v[:, half * LN:half * LN + LN]
        write_operand(a_ref, sv, h)
        return c

    lax.fori_loop(0, HE, row, 0)

    def out_copy(q, a, hp):
        return pltpu.make_async_copy(ob.at[q, a], out.at[:, 2 * (q * 3 + hp) + a], o_sem.at[q, a])

    def main(*accs):
        for acc in accs:
            pltpu.matmul_pop(acc)
        taps = [(a, b, k, l) for a in PAIR for b in PAIR for k in range(3) for l in range(3)]

        def push(i):
            _, _, k, l = taps[i]
            for q in PAIR:
                pltpu.matmul_push_rhs(wu[k, l], staging_register=0, mxu_index=q, transpose=True)

        def third(hp, c):
            push(0)
            for i, (a, b, k, l) in enumerate(taps):
                ph = (a * 2 + b) % 3
                dh = (a + k + 1) // 2
                kw = (b + l + 1) // 2
                for q in PAIR:
                    h = q * 3 + hp + dh
                    pltpu.matmul_acc_lhs(accs[q * 6 + ph * 2], a_ref[kw, h, pl.ds(32, NA), :], load_staged_rhs=0)
                    if i + 1 < len(taps):
                        _, _, k2, l2 = taps[i + 1]
                        pltpu.matmul_push_rhs(wu[k2, l2], staging_register=0, mxu_index=q, transpose=True)
                    pltpu.matmul_acc_lhs(accs[q * 6 + ph * 2 + 1], a_ref[kw, h, pl.ds(ABASE + 32, NB), :])
                if (k, l) != (2, 2):
                    continue
                for q in PAIR:
                    va = pltpu.matmul_pop(accs[q * 6 + ph * 2]) + ub[...]
                    vb = pltpu.matmul_pop(accs[q * 6 + ph * 2 + 1]) + ub[...]
                    for half in PAIR:
                        ln = slice(half * 128, half * 128 + 128)
                        for t in range(T):
                            o32[q, half, pl.ds(t * 48 + b, 16, stride=2), :] = va[t * 16:t * 16 + 16, ln]
                            kb = (t % T2) * 16 + (t // T2) * 8
                            o32[q, half, pl.ds(t * 48 + 32 + b, 8, stride=2), :] = vb[kb:kb + 8, ln]
                    if b == 1:
                        @pl.when(hp > 0)
                        def _(q=q, a=a):
                            out_copy(q, a, hp - 1).wait()
                        for t in range(T):
                            for half in PAIR:
                                ob[q, a, t, :, lanes(half)] = o32[q, half, pl.ds(t * 48, 48), :].astype(BF16)
                        out_copy(q, a, hp).start()
            return c

        lax.fori_loop(0, 3, third, 0)
        for q in PAIR:
            for a in PAIR:
                out_copy(q, a, 2).wait()

    pl.run_scoped(main, *acc_specs())


def solution(mesh):
    n_sh, n_sw = mesh.shape["sh"], mesh.shape["sw"]
    n_dev = n_sh * n_sw
    vmem = pl.BlockSpec(memory_space=pltpu.VMEM)
    hbm = pl.BlockSpec(memory_space=pl.ANY)
    dma = pltpu.SemaphoreType.DMA

    def local_step(features, latent, gn_gain, gn_bias, zy_weight, zy_bias, zb_weight, zb_bias, conv_weight, conv_bias, up_weight, up_bias):
        feat = features[0].transpose(1, 2, 3, 0)
        lat = latent[0].transpose(1, 2, 0, 3)
        cw = conv_weight.transpose(0, 1, 4, 5, 6, 2, 3).reshape(2, 2, 27, C, C)
        uw = up_weight.transpose(2, 3, 0, 1)
        xe, ce = pl.pallas_call(
            functools.partial(stage_kernel, n_sh, n_sw),
            out_shape=(jax.ShapeDtypeStruct((HE, T, W, C), BF16), jax.ShapeDtypeStruct((2, HE, 16, C), BF16)),
            in_specs=[hbm, hbm] + [vmem] * 6 + [hbm, vmem],
            out_specs=(vmem, vmem),
            scratch_shapes=[
                pltpu.VMEM((4, 27, C, C), BF16),
                pltpu.VMEM((3, HE, AR, C), BF16),
                pltpu.VMEM((2, HE * FR, 128), F32),
                pltpu.VMEM((H, FR, C), F32),
                pltpu.VMEM((H, FR, C), F32),
                pltpu.VMEM((HE + 1, FR, C), F32),
                pltpu.VMEM((HE + 1, FR, C), F32),
                pltpu.VMEM((HE + 1, FR, 128), BF16),
                pltpu.VMEM((H * FR + 96, 128), F32),
                pltpu.VMEM((T, H, LZ, W), BF16),
                pltpu.VMEM((T, H, W, C), BF16),
                pltpu.VMEM((5, 2, T, W, C), BF16),
                pltpu.VMEM((5, 2, HE, 16, C), BF16),
                pltpu.VMEM((2, T, W, C), BF16),
                pltpu.VMEM((2, H, 16, C), BF16),
                pltpu.VMEM((2, H * 16, 128), BF16),
                pltpu.VMEM((2, T * SW_, 128), F32),
                pltpu.VMEM((128, 2 * C), BF16),
                pltpu.VMEM((4, 8, 128), F32),
                pltpu.VMEM((4, n_dev, 8, 128), F32),
                pltpu.VMEM((3, 8, C), F32),
                dma((2,)), dma((4,)), dma((5, 8)), dma((5, 8)), dma((8,)), dma((8,)), dma((4, n_dev)), dma((4, n_dev)),
            ],
            compiler_params=pltpu.CompilerParams(collective_id=0, has_side_effects=True, vmem_limit_bytes=56 << 20),
            name="stages",
        )(feat, lat, gn_gain, gn_bias, zy_weight, zy_bias, zb_weight, zb_bias, cw, conv_bias)
        out = pl.pallas_call(
            up_kernel,
            out_shape=jax.ShapeDtypeStruct((T, 2 * H, 2 * W, C), BF16),
            in_specs=[vmem] * 4,
            out_specs=hbm,
            scratch_shapes=[
                pltpu.VMEM((3, HE, AR, C), BF16),
                pltpu.VMEM((2, T * SW_, 128), F32),
                pltpu.VMEM((2, 2, T * 2 * W, 128), F32),
                pltpu.VMEM((2, 2, T, 2 * W, C), BF16),
                dma((2, 2)),
            ],
            compiler_params=pltpu.CompilerParams(vmem_limit_bytes=40 << 20),
            name="upsample",
        )(xe, ce, uw, up_bias.reshape(1, C))
        return out.transpose(3, 0, 1, 2)[None]

    data_spec = P("dp", None, None, "sh", "sw")
    return jax.shard_map(local_step, mesh=mesh, in_specs=(data_spec, data_spec) + (P(),) * 10, out_specs=data_spec, check_vma=False)
```

time: 379 us -> 83.3 us (0.22); the launches traced: 373 us -> 82.4 us
  blocking collectives: 126 us -> 0 us
  Pallas kernels: 0 us -> 80.2 us
  matrix products: 78.4 us -> 0 us
  local copies, waits for them, and re-layouts: 76.8 us -> 2.17 us
  waiting for transfers between devices: 39.9 us -> 0 us
  starting transfers between devices: 37.9 us -> 0 us
  other arithmetic: 13 us -> 0 us
    psum x4 -> x0, blocking collectives: 126 us -> none  [group_norm(): total_stats = lax.psum(local_stats, ('sh', 'sw'))]
    pallas_call x0 -> x2, Pallas kernels: none -> 80.2 us  [the longest x1 68.6 us: local_step(): pl.pallas_call(functools.partial(stage_kernel, n_sh, n_sw), out_shape=(ja...]
    conv_general_dilated x5 -> x0, matrix products: 59.2 us -> none  [the longest x4 48.8 us: causal_conv(): lax.conv_general_dilated(padded, weight, (1, 1, 1), 'VALID', dimension_nu...]
    ppermute x20 -> x0, waiting for transfers between devices: 39.9 us -> none  [the longest x10 38.3 us: edge_exchange(): lax.ppermute(head, axis_name, [(i + 1, i) for i in range(n_dev - 1)])]
    ppermute x20 -> x0, starting transfers between devices: 37.9 us -> none  [the longest x10 24.2 us: edge_exchange(): lax.ppermute(tail, axis_name, [(i, i + 1) for i in range(n_dev - 1)])]
    convert_element_type x11 -> x0, local copies, waits for them, and re-layouts: 30.6 us -> none  [the longest x3 15.4 us: upsample_conv(): return (conv_out + per_channel(bias)).astype(jnp.bfloat16)]
    dot_general x8 -> x0, matrix products: 19.1 us -> none  [latent_map(): jnp.einsum('nzthw,zc->ncthw', latent, weight, preferred_element_type=jnp....]
    conv_general_dilated x14 -> x0, local copies, waits for them, and re-layouts: 18.1 us -> none  [the longest x12 15.3 us: causal_conv(): lax.conv_general_dilated(padded, weight, (1, 1, 1), 'VALID', dimension_nu...]
  transfers between devices with their start and end apart: 20 -> 0, of which waited for: 12 -> 0; matrix products, arithmetic and copies ran while one was open for 2% -> 0% of each run, Pallas kernels for 0% -> 0%
where the time goes in v1:
time: 83.3 us; the launch traced here: 82.4 us
  Pallas kernels  80.2 us (96%)
  local copies, waits for them, and re-layouts  2.17 us (3%)
    pallas_call x1, Pallas kernels, local_step(): pl.pallas_call(functools.partial(stage_kernel, n_sh, n_sw), out_shape=(ja...  68.6 us
    pallas_call x1, Pallas kernels, local_step(): pl.pallas_call(up_kernel, out_shape=jax.ShapeDtypeStruct((T, 2 * H, 2 * W...  11.6 us
    unnamed x8, local copies, waits for them, and re-layouts  2.17 us

profile of v1, /device:TPU:0, one launch (start us, length us, event | category | flops | bytes accessed | tf_op | source)
XLA Modules:
  0.0 82.4 jit_solution(2844539068443617933)
XLA Ops:
  0.0 0.0 copy-start
  0.0 0.0 copy-start.3
  0.0 68.6 %stages.1 = (bf16[8,12,24,256]{3,2,1,0:T(8,128)(2,1)}, bf16[2,8,16,256]{3,2,1,0:T(8,128)(2,1)}) custom-call(bf16[12,6,24,256]{3,2,1,0:T(8,128)(2,1)} %bitcast.17, bf16[12,6,16,24]{3,2,1,0:T(8,128)(2,1)} %bitcast.18, f32[2,2,256]{2,1,0:T(2,128)} %gain.1, f32[2,2,256]{2,1,0:T(2,128)} %gbias.1, bf16[2,2,16,256]{3,2,1,0:T(8,128)(2,1)} %zyw.1, f32[2,2,256]{2,1,0:T(2,128)} %zyb.1, ...), custom_call_target="tpu_custom_call" | custom-call | tf_op jit(solution)/shard_map/stages/pallas_call | solution.py:492
  68.6 0.0 copy-done
  68.7 0.0 copy-done.3
  68.7 0.0 copy-start.1
  68.7 1.3 %copy-done.1 = bf16[8,12,24,256]{3,2,1,0:T(8,128)(2,1)S(1)} copy-done((bf16[8,12,24,256]{3,2,1,0:T(8,128)(2,1)S(1)}, bf16[8,12,24,256]{3,2,1,0:T(8,128)(2,1)}, u32[]{:S(2)}) %copy-start.1) | copy-done | bytes 1179672
  69.9 0.0 copy-start.2
  69.9 0.9 %copy-done.2 = bf16[2,8,16,256]{3,2,1,0:T(8,128)(2,1)S(1)} copy-done((bf16[2,8,16,256]{3,2,1,0:T(8,128)(2,1)S(1)}, bf16[2,8,16,256]{3,2,1,0:T(8,128)(2,1)}, u32[]{:S(2)}) %copy-start.2) | copy-done | bytes 131096
  70.8 11.6 %upsample.1 = bf16[12,12,48,256]{3,2,1,0:T(8,128)(2,1)} custom-call(bf16[8,12,24,256]{3,2,1,0:T(8,128)(2,1)S(1)} %copy-done.1, bf16[2,8,16,256]{3,2,1,0:T(8,128)(2,1)S(1)} %copy-done.2, bf16[3,3,256,256]{3,2,1,0:T(8,128)(2,1)S(1)} %bitcast.14, f32[1,256]{1,0:T(1,128)S(1)} %bitcast.15), custom_call_target="tpu_custom_call" | custom-call | tf_op jit(solution)/shard_map/upsample/pallas_call | solution.py:524
Async XLA Ops:
  0.0 68.6 %copy-start = (bf16[256,256,3,3]{1,0,3,2:T(8,128)(2,1)S(1)}, bf16[256,256,3,3]{1,0,3,2:T(8,128)(2,1)}, u32[]{:S(2)}) copy-start(bf16[256,256,3,3]{1,0,3,2:T(8,128)(2,1)} %param.22) | copy-start | bytes 3538948
  0.0 68.7 %copy-start.3 = (f32[256]{0:T(256)S(1)}, f32[256]{0:T(256)}, u32[]{:S(2)}) copy-start(f32[256]{0:T(256)} %param.23) | copy-start | bytes 3076
  68.7 1.3 %copy-start.1 = (bf16[8,12,24,256]{3,2,1,0:T(8,128)(2,1)S(1)}, bf16[8,12,24,256]{3,2,1,0:T(8,128)(2,1)}, u32[]{:S(2)}) copy-start(bf16[8,12,24,256]{3,2,1,0:T(8,128)(2,1)} %get-tuple-element.7.xe) | copy-start | bytes 3538948
  69.9 0.9 %copy-start.2 = (bf16[2,8,16,256]{3,2,1,0:T(8,128)(2,1)S(1)}, bf16[2,8,16,256]{3,2,1,0:T(8,128)(2,1)}, u32[]{:S(2)}) copy-start(bf16[2,8,16,256]{3,2,1,0:T(8,128)(2,1)} %get-tuple-element.8.ce) | copy-start | bytes 393220

commit v2 on v1

--- a/solution.py
+++ b/solution.py
@@ -20,11 +20,14 @@
 ABASE = (T + 2) * 16
 SW_ = 40
 T2 = T // 2
+dirs = [(-1, 0), (1, 0), (0, -1), (0, 1), (-1, -1), (-1, 1), (1, -1), (1, 1)]
+ROW_DIRS, COL_DIRS = (0, 1, 4, 5, 6, 7), (2, 3)
+EDGE, INNER = (0, H - 1), range(1, H - 1)
 
 
 LN = 128
-PAIR = range(2)
-TR = 16
+PAIR, TRIO = range(2), range(3)
+TR, SUB = 16, 8
 
 
 def lanes(half):
@@ -42,7 +45,7 @@
 def acc_specs():
     specs = []
     for q in PAIR:
-        for _ in range(3):
+        for _ in TRIO:
             specs += [pltpu.ACC(q)((NA, C), F32), pltpu.ACC(q)((NB, C), F32)]
     return specs
 
@@ -50,7 +53,7 @@
 def write_operand(a_ref, s_ref, h):
     for half in PAIR:
         ln = lanes(half)
-        for kw in range(3):
+        for kw in TRIO:
             tails = []
             for t in range(T):
                 body = s_ref[half, pl.ds(t * SW_ + 7 + kw, 16), :].astype(BF16)
@@ -65,10 +68,10 @@
                 a_ref[kw, h, pl.ds(ABASE + i * TR, TR), ln] = both
 
 
-def stage_kernel(n_sh, n_sw, feat, lat, gain, gbias, zyw, zyb, zbw, zbb, cw, cb,
+def stage_kernel(n_sh, n_sw, feat, lat, gain_in, gbias_in, zyw_in, zyb_in, zbw_in, zbb_in, cw, cb_in,
                  xe_out, ce_out,
                  wv, a_ref, rx, xres, cv, yv, bv, lt, ltf, lv, fb, re, ce, rs, cs, lts, sv, wz,
-                 stat_out, stat_in, par,
+                 stat_out, stat_in, par, gain, gbias, zyw, zyb, zbw, zbb, cb,
                  ld_sem, w_sem, hs_sem, hr_sem, ls_sem, lr_sem, ss_sem, sr_sem):
     n_dev = n_sh * n_sw
     sh = lax.axis_index("sh")
@@ -78,8 +81,12 @@
 
     ld_feat = pltpu.make_async_copy(feat, fb, ld_sem.at[0])
     ld_lat = pltpu.make_async_copy(lat, lv, ld_sem.at[1])
+    ld_lat.start()
     ld_feat.start()
-    ld_lat.start()
+    params = ((gain_in, gain), (gbias_in, gbias), (zyw_in, zyw), (zyb_in, zyb), (zbw_in, zbw), (zbb_in, zbb), (cb_in, cb))
+    ld_params = [pltpu.make_async_copy(src, dst, ld_sem.at[2 + i]) for i, (src, dst) in enumerate(params)]
+    for ld in ld_params:
+        ld.start()
 
     def ld_weight(n, b, s):
         return pltpu.make_async_copy(cw.at[b, s], wv.at[n], w_sem.at[n])
@@ -99,7 +106,6 @@
     for j in range(1, n_dev):
         pl.semaphore_signal(bar, inc=1, device_id=peer_of(j)[1], device_id_type=MESH)
 
-    dirs = [(-1, 0), (1, 0), (0, -1), (0, 1), (-1, -1), (-1, 1), (1, -1), (1, 1)]
 
     def exists(dy, dx):
         c = None
@@ -144,8 +150,9 @@
         return pltpu.make_async_remote_copy(src_ref=src, dst_ref=dst, send_sem=ls_sem.at[d],
                                             recv_sem=lr_sem.at[d], device_id=device(dy, dx), device_id_type=MESH)
 
-    def for_dirs(make, what):
-        for d, (dy, dx) in enumerate(dirs):
+    def for_dirs(make, what, which=ROW_DIRS + COL_DIRS):
+        for d in which:
+            dy, dx = dirs[d]
             if what == "recv":
                 @pl.when(exists(-dy, -dx))
                 def _(d=d):
@@ -200,21 +207,36 @@
         rstd = lax.rsqrt(var + GN_EPSILON)
         mean = jnp.concatenate([mean[0:1], mean[1:2]], axis=1)
         rstd = jnp.concatenate([rstd[0:1], rstd[1:2]], axis=1)
-        par[0] = jnp.broadcast_to(mean, (8, C))
-        par[1] = jnp.broadcast_to(rstd * chan(gain, b, s), (8, C))
-        par[2] = jnp.broadcast_to(chan(gbias, b, s), (8, C))
-
-    def fill_columns():
+        par[0] = jnp.broadcast_to(mean, (SUB, C))
+        par[1] = jnp.broadcast_to(rstd * chan(gain, b, s), (SUB, C))
+        par[2] = jnp.broadcast_to(chan(gbias, b, s), (SUB, C))
+
+    def fill_columns(rows):
+        for h in rows:
+            for side, w in ((0, 0), (1, W - 1)):
+                for half in PAIR:
+                    v = rx[half, pl.ds((h + 1) * FR + w, TR, stride=W), :]
+                    cs[side, h, :, lanes(half)] = v.astype(BF16)
+
+    def main():
+        wz[...] = jnp.zeros(wz.shape, BF16)
+        ltf[...] = jnp.zeros(ltf.shape, F32)
+        ld_lat.wait()
+
+        def turn_row(h, c):
+            for t in range(T):
+                ltf[pl.ds(h * FR + t * W, W), pl.ds(0, LZ)] = lv[t, h].astype(F32).T
+            lt[h + 1] = ltf[pl.ds(pl.multiple_of(h * FR, TR), FR), :].astype(BF16)
+            return c
+
+        lax.fori_loop(0, H, turn_row, 0)
         for h in range(H):
             for side, w in ((0, 0), (1, W - 1)):
-                for half in PAIR:
-                    v = rx[half, pl.ds((h + 1) * FR + w, 16, stride=W), :]
-                    cs[side, h, :, lanes(half)] = v.astype(BF16)
-
-    def main():
+                lts[side, tile(h), :] = ltf[pl.ds(h * FR + w, TR, stride=W), :].astype(BF16)
+
         ld_feat.wait()
         pivot0 = fb[0, 0, pl.ds(0, 8), :].astype(F32)[0:1, :]
-        pivot8 = jnp.broadcast_to(pivot0, (8, C))
+        pivot8 = jnp.broadcast_to(pivot0, (SUB, C))
 
         def load_row(h, carry):
             s1, s2 = carry
@@ -223,39 +245,25 @@
                 for half in PAIR:
                     rx[half, pl.ds((h + 1) * FR + t * W, W), :] = x[:, half * LN:half * LN + LN]
                 xres[h, pl.ds(t * W, W), :] = x
-                for i in range(3):
-                    d = x[i * 8:i * 8 + 8] - pivot8
+                for i in TRIO:
+                    d = x[i * SUB:i * SUB + SUB] - pivot8
                     s1 = s1 + d
                     s2 = s2 + d * d
             return s1, s2
 
-        zero8 = jnp.zeros((8, C), F32)
+        zero8 = jnp.zeros((SUB, C), F32)
         s1, s2 = lax.fori_loop(0, H, load_row, (zero8, zero8))
         for t in range(T):
             rs[0, t] = fb[t, 0]
             rs[1, t] = fb[t, H - 1]
-        fill_columns()
+        fill_columns(range(H))
+        row_src = (rs.at[0], rs.at[1])
         pl.semaphore_wait(bar, n_dev - 1)
         send_stats(0, pivot0, s1, s2)
-        row_src = (rs.at[0], rs.at[1])
+        for_dirs(lat_copy, "start")
         for_dirs(lambda d: halo_copy(0, d, row_src), "start")
-
-        ltf[...] = jnp.zeros(ltf.shape, F32)
-        ld_lat.wait()
-
-        def turn_row(h, c):
-            for t in range(T):
-                ltf[pl.ds(h * FR + t * W, W), pl.ds(0, LZ)] = lv[t, h].astype(F32).T
-            row = ltf[pl.ds(pl.multiple_of(h * FR, 16), FR), :].astype(BF16)
-            lt[h + 1] = row
-            return c
-
-        lax.fori_loop(0, H, turn_row, 0)
-        for h in range(H):
-            for side, w in ((0, 0), (1, W - 1)):
-                lts[side, tile(h), :] = ltf[pl.ds(h * FR + w, 16, stride=W), :].astype(BF16)
-        for_dirs(lat_copy, "start")
-        wz[...] = jnp.zeros(wz.shape, BF16)
+        for ld in ld_params:
+            ld.wait()
         for_dirs(lat_copy, "recv")
         for_dirs(lat_copy, "send")
 
@@ -318,53 +326,50 @@
 
             lax.fori_loop(0, HE, row, 0)
 
-        def conv(n):
+        def conv(n, rows, steps):
             def lhs(h, part, tap):
                 kt, kh, kw = tap // 9, tap // 3 % 3, tap % 3
                 return a_ref[kw, h + kh, pl.ds(kt * 16 + (ABASE if part else 0), NB if part else NA), :]
 
-            for i in range(9):
-                rhs = jnp.concatenate([wv[n, i * 3 + kw] for kw in range(3)], axis=1)
-                for h in range(H):
-                    cols = [jnp.concatenate([lhs(h, part, i * 3 + kw) for part in PAIR], axis=0) for kw in range(3)]
+            for i in steps:
+                rhs = jnp.concatenate([wv[n, i * 3 + kw] for kw in TRIO], axis=1)
+                for h in rows:
+                    cols = [jnp.concatenate([lhs(h, part, i * 3 + kw) for part in PAIR], axis=0) for kw in TRIO]
                     v = lax.dot_general(jnp.concatenate(cols, axis=1), rhs, CONTRACT_LAST, preferred_element_type=F32)
                     if i == 0:
                         cv[h] = v
                     else:
                         cv[h] += v
 
-        def finish(b, s):
+        def finish(b, s, rows, sums):
             bias = chan(cb, b, s)
-            pivot = None
-            s1 = s2 = zero8
-            for hh in range(3):
-                for q in PAIR:
-                    h = q * 3 + hh
-                    for part in PAIR:
-                        v = (cv[h, pl.ds(NA if part else 0, NB if part else NA), :] + bias).astype(BF16).astype(F32)
-                        nblk = 16 if part == 0 else 8
-                        for i in range(T):
-                            if part == 0:
-                                t, w0 = i, 0
-                            else:
-                                t, w0 = (i // 2) + (i % 2) * T2, 16
-                            blk = v[i * nblk:(i + 1) * nblk]
-                            r0 = t * W + w0
-                            if s == 1:
-                                blk = (blk + xres[h, pl.ds(r0, nblk), :]).astype(BF16).astype(F32)
-                                xres[h, pl.ds(r0, nblk), :] = blk
-                            for half in PAIR:
-                                rx[half, pl.ds((h + 1) * FR + r0, nblk), :] = blk[:, half * LN:half * LN + LN]
-                            if h in (0, H - 1):
-                                rs[0 if h == 0 else 1, t, pl.ds(w0, nblk), :] = blk.astype(BF16)
-                            if s == 1:
-                                xe_out[h + 1, t, pl.ds(w0, nblk), :] = blk.astype(BF16)
-                            if pivot is None:
-                                pivot = blk[0:1, :]
-                            for k in range(nblk // 8):
-                                d = blk[k * 8:k * 8 + 8] - pivot
-                                s1 = s1 + d
-                                s2 = s2 + d * d
+            pivot, s1, s2 = sums
+            for h in rows:
+                for part in PAIR:
+                    v = (cv[h, pl.ds(NA if part else 0, NB if part else NA), :] + bias).astype(BF16).astype(F32)
+                    nblk = 16 if part == 0 else 8
+                    for i in range(T):
+                        if part == 0:
+                            t, w0 = i, 0
+                        else:
+                            t, w0 = (i // 2) + (i % 2) * T2, 16
+                        blk = v[i * nblk:(i + 1) * nblk]
+                        r0 = t * W + w0
+                        if s == 1:
+                            blk = (blk + xres[h, pl.ds(r0, nblk), :]).astype(BF16).astype(F32)
+                            xres[h, pl.ds(r0, nblk), :] = blk
+                        for half in PAIR:
+                            rx[half, pl.ds((h + 1) * FR + r0, nblk), :] = blk[:, half * LN:half * LN + LN]
+                        if h in (0, H - 1):
+                            rs[0 if h == 0 else 1, t, pl.ds(w0, nblk), :] = blk.astype(BF16)
+                        if s == 1:
+                            xe_out[h + 1, t, pl.ds(w0, nblk), :] = blk.astype(BF16)
+                        if pivot is None:
+                            pivot = blk[0:1, :]
+                        for k in range(nblk // 8):
+                            d = blk[k * SUB:k * SUB + SUB] - pivot
+                            s1 = s1 + d
+                            s2 = s2 + d * d
             return pivot, s1, s2
 
         def block(b, carry):
@@ -376,17 +381,22 @@
                 recv_stats(n, b, s)
                 activate_rows(n)
                 ld_weight(n, b, s).wait()
-                conv(n)
                 for_dirs(lambda d: halo_copy(n, d, row_src), "send")
-                pivot, s1, s2 = finish(b, s)
+                conv(n, EDGE, range(9))
+                sums = finish(b, s, EDGE, (None, zero8, zero8))
+                fill_columns(EDGE)
+                conv(n, INNER, PAIR)
+                for_dirs(lambda d: halo_copy(n + 1, d, row_src), "start", ROW_DIRS)
+                conv(n, INNER, range(2, 9))
+                pivot, s1, s2 = finish(b, s, INNER, sums)
                 if s == 0:
                     send_stats(n + 1, pivot, s1, s2)
                 else:
                     @pl.when(b == 0)
                     def _():
                         send_stats(n + 1, pivot, s1, s2)
-                fill_columns()
-                for_dirs(lambda d: halo_copy(n + 1, d, row_src), "start")
+                fill_columns(INNER)
+                for_dirs(lambda d: halo_copy(n + 1, d, row_src), "start", COL_DIRS)
             return carry
 
         lax.fori_loop(0, 2, block, 0)
@@ -407,7 +417,7 @@
     main()
 
 
-def up_kernel(xe, ce, wu, ub, out, a_ref, sv, o32, ob, o_sem):
+def up_kernel(xe, ce, wu, ub, out, a_ref, sv, o32, part, ob, o_sem):
     def row(h, c):
         for side in PAIR:
             v = ce[side, h].astype(F32)
@@ -423,56 +433,72 @@
     lax.fori_loop(0, HE, row, 0)
 
     def out_copy(q, a, hp):
-        return pltpu.make_async_copy(ob.at[q, a], out.at[:, 2 * (q * 3 + hp) + a], o_sem.at[q, a])
+        return pltpu.make_async_copy(ob.at[hp, q, a], out.at[:, 2 * (q * 3 + hp) + a], o_sem.at[hp, q, a])
 
     def main(*accs):
         for acc in accs:
             pltpu.matmul_pop(acc)
-        taps = [(a, b, k, l) for a in PAIR for b in PAIR for k in range(3) for l in range(3)]
+
+        def row_taps(a):
+            return [(1, 1)] if a is None else [(0, a), (2, a + 1)]
+
+        groups = []
+        for a in (None, 0, 1):
+            for b in (None, 0, 1):
+                groups.append((a, b, [(k, l, dh, kw) for k, dh in row_taps(a) for l, kw in row_taps(b)]))
+        taps = [(g, tap) for g, grp in enumerate(groups) for tap in grp[2]]
 
         def push(i):
-            _, _, k, l = taps[i]
+            k, l, _, _ = taps[i % len(taps)][1]
             for q in PAIR:
                 pltpu.matmul_push_rhs(wu[k, l], staging_register=0, mxu_index=q, transpose=True)
 
-        def third(hp, c):
-            push(0)
-            for i, (a, b, k, l) in enumerate(taps):
-                ph = (a * 2 + b) % 3
-                dh = (a + k + 1) // 2
-                kw = (b + l + 1) // 2
+        def blocks(q, slot):
+            va = pltpu.matmul_pop(accs[q * 6 + slot * 2])
+            vb = pltpu.matmul_pop(accs[q * 6 + slot * 2 + 1])
+            return va, vb
+
+        push(0)
+        for hp in TRIO:
+            for i, (g, (k, l, dh, kw)) in enumerate(taps):
+                slot = g % 3
                 for q in PAIR:
-                    h = q * 3 + hp + dh
-                    pltpu.matmul_acc_lhs(accs[q * 6 + ph * 2], a_ref[kw, h, pl.ds(32, NA), :], load_staged_rhs=0)
-                    if i + 1 < len(taps):
-                        _, _, k2, l2 = taps[i + 1]
-                        pltpu.matmul_push_rhs(wu[k2, l2], staging_register=0, mxu_index=q, transpose=True)
-                    pltpu.matmul_acc_lhs(accs[q * 6 + ph * 2 + 1], a_ref[kw, h, pl.ds(ABASE + 32, NB), :])
-                if (k, l) != (2, 2):
+                    pltpu.matmul_acc_lhs(accs[q * 6 + slot * 2], a_ref[kw, q * 3 + hp + dh, pl.ds(32, NA), :], load_staged_rhs=0)
+                if hp < 2 or i + 1 < len(taps):
+                    push(i + 1)
+                for q in PAIR:
+                    pltpu.matmul_acc_lhs(accs[q * 6 + slot * 2 + 1], a_ref[kw, q * 3 + hp + dh, pl.ds(ABASE + 32, NB), :])
+                if i + 1 < len(taps) and taps[i + 1][0] == g:
                     continue
+                a, b, _ = groups[g]
                 for q in PAIR:
-                    va = pltpu.matmul_pop(accs[q * 6 + ph * 2]) + ub[...]
-                    vb = pltpu.matmul_pop(accs[q * 6 + ph * 2 + 1]) + ub[...]
+                    va, vb = blocks(q, slot)
+                    for v, sl in ((va, pl.ds(0, NA)), (vb, pl.ds(NA, NB))):
+                        if a is None and b is None:
+                            part[q, 0, sl, :] = v + ub[...]
+                        elif a is None:
+                            part[q, 1 + b, sl, :] = v + part[q, 0, sl, :]
+                        elif b is None:
+                            part[q, 3, sl, :] = v
+                    if a is None or b is None:
+                        continue
+                    va = va + part[q, 1 + b, pl.ds(0, NA), :] + part[q, 3, pl.ds(0, NA), :]
+                    vb = vb + part[q, 1 + b, pl.ds(NA, NB), :] + part[q, 3, pl.ds(NA, NB), :]
                     for half in PAIR:
-                        ln = slice(half * 128, half * 128 + 128)
+                        ln = slice(half * LN, half * LN + LN)
                         for t in range(T):
-                            o32[q, half, pl.ds(t * 48 + b, 16, stride=2), :] = va[t * 16:t * 16 + 16, ln]
-                            kb = (t % T2) * 16 + (t // T2) * 8
+                            o32[q, half, pl.ds(t * 2 * W + b, TR, stride=2), :] = va[t * TR:t * TR + TR, ln]
+                            kb = (t % T2) * TR + (t // T2) * 8
                             o32[q, half, pl.ds(t * 48 + 32 + b, 8, stride=2), :] = vb[kb:kb + 8, ln]
                     if b == 1:
-                        @pl.when(hp > 0)
-                        def _(q=q, a=a):
-                            out_copy(q, a, hp - 1).wait()
                         for t in range(T):
                             for half in PAIR:
-                                ob[q, a, t, :, lanes(half)] = o32[q, half, pl.ds(t * 48, 48), :].astype(BF16)
+                                ob[hp, q, a, t, :, lanes(half)] = o32[q, half, pl.ds(t * 2 * W, 2 * W), :].astype(BF16)
                         out_copy(q, a, hp).start()
-            return c
-
-        lax.fori_loop(0, 3, third, 0)
-        for q in PAIR:
-            for a in PAIR:
-                out_copy(q, a, 2).wait()
+        for hp in TRIO:
+            for q in PAIR:
+                for a in PAIR:
+                    out_copy(q, a, hp).wait()
 
     pl.run_scoped(main, *acc_specs())
 
@@ -481,8 +507,9 @@
     n_sh, n_sw = mesh.shape["sh"], mesh.shape["sw"]
     n_dev = n_sh * n_sw
     vmem = pl.BlockSpec(memory_space=pltpu.VMEM)
-    hbm = pl.BlockSpec(memory_space=pl.ANY)
+    hbm = pl.BlockSpec(memory_space=pltpu.HBM)
     dma = pltpu.SemaphoreType.DMA
+    vec, mat = pltpu.VMEM((2, 2, C), F32), pltpu.VMEM((2, 2, LZ, C), BF16)
 
     def local_step(features, latent, gn_gain, gn_bias, zy_weight, zy_bias, zb_weight, zb_bias, conv_weight, conv_bias, up_weight, up_bias):
         feat = features[0].transpose(1, 2, 3, 0)
@@ -492,7 +519,7 @@
         xe, ce = pl.pallas_call(
             functools.partial(stage_kernel, n_sh, n_sw),
             out_shape=(jax.ShapeDtypeStruct((HE, T, W, C), BF16), jax.ShapeDtypeStruct((2, HE, 16, C), BF16)),
-            in_specs=[hbm, hbm] + [vmem] * 6 + [hbm, vmem],
+            in_specs=[hbm] * 10,
             out_specs=(vmem, vmem),
             scratch_shapes=[
                 pltpu.VMEM((4, 27, C, C), BF16),
@@ -516,11 +543,12 @@
                 pltpu.VMEM((4, 8, 128), F32),
                 pltpu.VMEM((4, n_dev, 8, 128), F32),
                 pltpu.VMEM((3, 8, C), F32),
-                dma((2,)), dma((4,)), dma((5, 8)), dma((5, 8)), dma((8,)), dma((8,)), dma((4, n_dev)), dma((4, n_dev)),
+                vec, vec, mat, vec, mat, vec, vec,
+                dma((9,)), dma((4,)), dma((5, 8)), dma((5, 8)), dma((8,)), dma((8,)), dma((4, n_dev)), dma((4, n_dev)),
             ],
-            compiler_params=pltpu.CompilerParams(collective_id=0, has_side_effects=True, vmem_limit_bytes=56 << 20),
+            compiler_params=pltpu.CompilerParams(collective_id=0, has_side_effects=True, vmem_limit_bytes=40 << 20),
             name="stages",
-        )(feat, lat, gn_gain, gn_bias, zy_weight, zy_bias, zb_weight, zb_bias, cw, conv_bias)
+        )(*[pltpu.with_memory_space_constraint(v, pltpu.HBM) for v in (feat, lat, gn_gain, gn_bias, zy_weight, zy_bias, zb_weight, zb_bias, cw, conv_bias)])
         out = pl.pallas_call(
             up_kernel,
             out_shape=jax.ShapeDtypeStruct((T, 2 * H, 2 * W, C), BF16),
@@ -530,8 +558,9 @@
                 pltpu.VMEM((3, HE, AR, C), BF16),
                 pltpu.VMEM((2, T * SW_, 128), F32),
                 pltpu.VMEM((2, 2, T * 2 * W, 128), F32),
-                pltpu.VMEM((2, 2, T, 2 * W, C), BF16),
-                dma((2, 2)),
+                pltpu.VMEM((2, 4, FR, C), F32),
+                pltpu.VMEM((3, 2, 2, T, 2 * W, C), BF16),
+                dma((3, 2, 2)),
             ],
             compiler_params=pltpu.CompilerParams(vmem_limit_bytes=40 << 20),
             name="upsample",

time: 83.3 us -> 71.5 us (0.86)
  Pallas kernels: 80.2 us -> 71.2 us
  local copies, waits for them, and re-layouts: 2.17 us -> 0.01 us
    pallas_call x1, Pallas kernels: 68.6 us -> 62.2 us  [local_step(): pl.pallas_call(functools.partial(stage_kernel, n_sh, n_sw), out_shape=(ja...]
    pallas_call x1, Pallas kernels: 11.6 us -> 8.98 us  [local_step(): pl.pallas_call(up_kernel, out_shape=jax.ShapeDtypeStruct((T, 2 * H, 2 * W...]
    unnamed x8 -> x4, local copies, waits for them, and re-layouts: 2.17 us -> 0.01 us
where the time goes in v2:
time: 71.5 us; the launch traced here: 71.4 us
  Pallas kernels  71.2 us (100%)
    pallas_call x1, Pallas kernels, local_step(): pl.pallas_call(functools.partial(stage_kernel, n_sh, n_sw), out_shape=(ja...  62.2 us
    pallas_call x1, Pallas kernels, local_step(): pl.pallas_call(up_kernel, out_shape=jax.ShapeDtypeStruct((T, 2 * H, 2 * W...  8.98 us

profile of v2, /device:TPU:0, one launch (start us, length us, event | category | flops | bytes accessed | tf_op | source)
XLA Modules:
  0.0 71.4 jit_solution(12270012834455540355)
XLA Ops:
  0.0 0.0 copy-start
  0.0 0.0 copy-start.1
  0.0 62.2 %stages.1 = (bf16[8,12,24,256]{3,2,1,0:T(8,128)(2,1)S(1)}, bf16[2,8,16,256]{3,2,1,0:T(8,128)(2,1)S(1)}) custom-call(bf16[12,6,24,256]{3,2,1,0:T(8,128)(2,1)} %bitcast.17, bf16[12,6,16,24]{3,2,1,0:T(8,128)(2,1)} %bitcast.18, f32[2,2,256]{2,1,0:T(2,128)} %gain_in.1, f32[2,2,256]{2,1,0:T(2,128)} %gbias_in.1, bf16[2,2,16,256]{3,2,1,0:T(8,128)(2,1)} %zyw_in.1, ...), custom_call_target="tpu_custom_call" | custom-call | tf_op jit(solution)/shard_map/stages/pallas_call | solution.py:519
  62.2 0.0 copy-done
  62.2 0.0 copy-done.1
  62.2 9.0 %upsample.1 = bf16[12,12,48,256]{3,2,1,0:T(8,128)(2,1)} custom-call(bf16[8,12,24,256]{3,2,1,0:T(8,128)(2,1)S(1)} %get-tuple-element.7.xe, bf16[2,8,16,256]{3,2,1,0:T(8,128)(2,1)S(1)} %get-tuple-element.8.ce, bf16[3,3,256,256]{3,2,1,0:T(8,128)(2,1)S(1)} %bitcast.14, f32[1,256]{1,0:T(1,128)S(1)} %bitcast.15), custom_call_target="tpu_custom_call" | custom-call | tf_op jit(solution)/shard_map/upsample/pallas_call | solution.py:552
Async XLA Ops:
  0.0 62.2 %copy-start = (bf16[256,256,3,3]{1,0,3,2:T(8,128)(2,1)S(1)}, bf16[256,256,3,3]{1,0,3,2:T(8,128)(2,1)}, u32[]{:S(2)}) copy-start(bf16[256,256,3,3]{1,0,3,2:T(8,128)(2,1)} %param.22) | copy-start | bytes 3538948
  0.0 62.2 %copy-start.1 = (f32[256]{0:T(256)S(1)}, f32[256]{0:T(256)}, u32[]{:S(2)}) copy-start(f32[256]{0:T(256)} %param.23) | copy-start | bytes 3076

commit v3 on v2

--- a/solution.py
+++ b/solution.py
@@ -27,6 +27,7 @@
 
 LN = 128
 PAIR, TRIO = range(2), range(3)
+GAPS = (1, 2, 4)
 TR, SUB = 16, 8
 
 
@@ -50,18 +51,18 @@
     return specs
 
 
-def write_operand(a_ref, s_ref, h):
+def write_operand(a_ref, s_ref, h, body_kw=TRIO, tail_kw=TRIO):
     for half in PAIR:
         ln = lanes(half)
-        for kw in TRIO:
-            tails = []
+        for kw in body_kw:
             for t in range(T):
-                body = s_ref[half, pl.ds(t * SW_ + 7 + kw, 16), :].astype(BF16)
+                body = s_ref[h, half, pl.ds(t * SW_ + 7 + kw, TR), :].astype(BF16)
                 a_ref[kw, h, tile(t + 2), ln] = body
                 if t == 0:
                     a_ref[kw, h, tile(0), ln] = body
                     a_ref[kw, h, tile(1), ln] = body
-                tails.append(s_ref[half, pl.ds(t * SW_ + 23 + kw, 8), :])
+        for kw in tail_kw:
+            tails = [s_ref[h, half, pl.ds(t * SW_ + 23 + kw, SUB), :] for t in range(T)]
             pairs = [(max(t, 0), t + T2) for t in range(-2, T2)]
             for i, (p, n) in enumerate(pairs):
                 both = jnp.concatenate([tails[p], tails[n]], axis=0).astype(BF16)
@@ -69,7 +70,7 @@
 
 
 def stage_kernel(n_sh, n_sw, feat, lat, gain_in, gbias_in, zyw_in, zyb_in, zbw_in, zbb_in, cw, cb_in,
-                 xe_out, ce_out,
+                 aup,
                  wv, a_ref, rx, xres, cv, yv, bv, lt, ltf, lv, fb, re, ce, rs, cs, lts, sv, wz,
                  stat_out, stat_in, par, gain, gbias, zyw, zyb, zbw, zbb, cb,
                  ld_sem, w_sem, hs_sem, hr_sem, ls_sem, lr_sem, ss_sem, sr_sem):
@@ -170,43 +171,48 @@
         return pltpu.make_async_remote_copy(src_ref=stat_out.at[n], dst_ref=stat_in.at[n, me], send_sem=ss_sem.at[n, j],
                                             recv_sem=sr_sem.at[n, me], device_id=dev, device_id_type=MESH)
 
+    lane = lax.broadcasted_iota(jnp.int32, (1, LN), 1) & 7
+
+    def partner(v, gap):
+        return jnp.where((lane & gap) == 0, pltpu.roll(v, LN - gap, 1), pltpu.roll(v, gap, 1))
+
+    def stack(v):
+        return jnp.concatenate([v[:, :LN], v[:, LN:]], axis=0)
+
     def send_stats(n, pivot, s1, s2):
-        count = float(T * H * W)
-        s1 = jnp.sum(s1, axis=0, keepdims=True) * (1.0 / count)
-        s2 = jnp.sum(s2, axis=0, keepdims=True) * (1.0 / count)
-        mean = pivot + s1
-        var = jnp.maximum(s2 - s1 * s1, 0.0)
-        rows = [mean[:, :128], mean[:, 128:], var[:, :128], var[:, 128:]]
-        packed = jnp.concatenate(rows + [jnp.zeros((4, 128), F32)], axis=0)
-        stat_out[n] = packed
-        stat_in[n, me] = packed
-        for j in range(1, n_dev):
-            stat_copy(n, j).start()
-
-    def recv_stats(n, b, s):
-        for j in range(1, n_dev):
-            p = lax.rem(me + j, n_dev)
-            pltpu.make_async_remote_copy(src_ref=stat_out.at[n], dst_ref=stat_in.at[n, p], send_sem=ss_sem.at[n, j],
-                                         recv_sem=sr_sem.at[n, p], device_id=peer_of(j)[1], device_id_type=MESH).wait_recv()
-        vals = [stat_in[n, i] for i in range(n_dev)]
-        total = functools.reduce(jnp.add, vals) * (1.0 / n_dev)
-        mean = total[0:2, :]
-        dev = functools.reduce(jnp.add, [jnp.square(v[0:2, :] - mean) for v in vals]) * (1.0 / n_dev)
-        var = total[2:4, :] + dev
-        lane = lax.broadcasted_iota(jnp.int32, (2, 128), 1)
-        for gap in (1, 2, 4):
-            low = (lane & gap) == 0
-
-            def partner(v):
-                return jnp.where(low, pltpu.roll(v, LN - gap, 1), pltpu.roll(v, gap, 1))
-
-            mp, vp = partner(mean), partner(var)
+        count = 1.0 / (T * H * W)
+        s1 = jnp.sum(s1, axis=0, keepdims=True) * count
+        s2 = jnp.sum(s2, axis=0, keepdims=True) * count
+        mean, var = stack(pivot + s1), stack(jnp.maximum(s2 - s1 * s1, 0.0))
+        for gap in GAPS:
+            mp, vp = partner(mean, gap), partner(var, gap)
             half_gap = (mean - mp) * 0.5
             var = (var + vp) * 0.5 + half_gap * half_gap
             mean = (mean + mp) * 0.5
-        rstd = lax.rsqrt(var + GN_EPSILON)
-        mean = jnp.concatenate([mean[0:1], mean[1:2]], axis=1)
-        rstd = jnp.concatenate([rstd[0:1], rstd[1:2]], axis=1)
+        quad = (mean[0:1], mean[1:2], var[0:1], var[1:2])
+        row = sum(jnp.where(lane == i, v, 0.0) for i, v in enumerate(quad))
+        stat_out[n] = row
+        stat_in[n, me] = row
+        for j in range(1, n_dev):
+            stat_copy(n, j).start()
+
+    def recv_stats(n, b, s):
+        for j in range(1, n_dev):
+            p, dev = peer_of(j)
+            pltpu.make_async_remote_copy(src_ref=stat_out.at[n], dst_ref=stat_in.at[n, p], send_sem=ss_sem.at[n, j],
+                                         recv_sem=sr_sem.at[n, p], device_id=dev, device_id_type=MESH).wait_recv()
+        vals = [stat_in[n, i] for i in range(n_dev)]
+        total = functools.reduce(jnp.add, vals) * (1.0 / n_dev)
+        between = functools.reduce(jnp.add, [jnp.square(v - total) for v in vals]) * (1.0 / n_dev)
+
+        def pick(v, i):
+            return jnp.where(lane == i, v, 0.0)
+
+        x = jnp.concatenate([pick(total, 0), pick(total, 1), pick(total, 2) + pick(between, 0), pick(total, 3) + pick(between, 1)], axis=0)
+        for gap in GAPS:
+            x = x + partner(x, gap)
+        mean = jnp.concatenate([x[0:1], x[1:2]], axis=1)
+        rstd = lax.rsqrt(jnp.concatenate([x[2:3], x[3:4]], axis=1) + GN_EPSILON)
         par[0] = jnp.broadcast_to(mean, (SUB, C))
         par[1] = jnp.broadcast_to(rstd * chan(gain, b, s), (SUB, C))
         par[2] = jnp.broadcast_to(chan(gbias, b, s), (SUB, C))
@@ -309,22 +315,40 @@
             cond = jnp.logical_and(cond, jnp.logical_or(h < HE - 1, has["d"]))
             return jnp.where(cond, ce[e, side, h].astype(F32), 0.0)
 
+        def put_column(h, side, v):
+            for half in PAIR:
+                sv[h, half, pl.ds(7 + side * 25, T, stride=SW_), :] = v[0:T, half * LN:half * LN + LN]
+
+        def own_rows(h, t, half):
+            return rx[half, pl.ds(pl.multiple_of(h * FR, SUB) + t * W, W), :]
+
         def activate_rows(n):
             def row(h, c):
                 for side in PAIR:
-                    k = side * 128 + h * 16
-                    v = activate(col_vals(n, side, h), yv[HE, pl.ds(pl.multiple_of(k, TR), TR), :], bv[HE, pl.ds(pl.multiple_of(k, TR), TR), :])
-                    for half in PAIR:
-                        sv[half, pl.ds(7 + side * 25, T, stride=SW_), :] = v[0:T, half * LN:half * LN + LN]
+                    at = pl.ds(pl.multiple_of(side * LN + h * TR, TR), TR)
+                    put_column(h, side, activate(col_vals(n, side, h), yv[HE, at, :], bv[HE, at, :]))
                 for t in range(T):
-                    x = jnp.concatenate([rx[half, pl.ds(pl.multiple_of(h * FR, 8) + t * W, W), :] for half in PAIR], axis=1)
+                    x = jnp.concatenate([own_rows(h, t, half) for half in PAIR], axis=1)
                     v = activate(x, yv[h, pl.ds(t * W, W), :], bv[h, pl.ds(t * W, W), :])
                     for half in PAIR:
-                        sv[half, pl.ds(t * SW_ + 8, W), :] = v[:, half * LN:half * LN + LN]
+                        sv[h, half, pl.ds(t * SW_ + 8, W), :] = v[:, half * LN:half * LN + LN]
                 write_operand(a_ref, sv, h)
                 return c
 
             lax.fori_loop(0, HE, row, 0)
+
+        def plain_row(h, c):
+            for t in range(T):
+                for half in PAIR:
+                    sv[h, half, pl.ds(t * SW_ + 8, W), :] = own_rows(h, t, half)
+            write_operand(aup, sv, h)
+            return c
+
+        def plain_edges(h, c):
+            for side in PAIR:
+                put_column(h, side, col_vals(4, side, h))
+            write_operand(aup, sv, h, (0,), (2,))
+            return c
 
         def conv(n, rows, steps):
             def lhs(h, part, tap):
@@ -362,8 +386,6 @@
                             rx[half, pl.ds((h + 1) * FR + r0, nblk), :] = blk[:, half * LN:half * LN + LN]
                         if h in (0, H - 1):
                             rs[0 if h == 0 else 1, t, pl.ds(w0, nblk), :] = blk.astype(BF16)
-                        if s == 1:
-                            xe_out[h + 1, t, pl.ds(w0, nblk), :] = blk.astype(BF16)
                         if pivot is None:
                             pivot = blk[0:1, :]
                         for k in range(nblk // 8):
@@ -401,14 +423,13 @@
 
         lax.fori_loop(0, 2, block, 0)
 
-        for_dirs(lambda d: halo_copy(4, d, row_src), "recv")
-        for i, cond in ((0, has["u"]), (1, has["d"])):
-            row = 0 if i == 0 else HE - 1
-            for t in range(T):
-                xe_out[row, t] = jnp.where(cond, re[4, i, t].astype(F32), 0.0).astype(BF16)
-        for side in PAIR:
-            for h in range(HE):
-                ce_out[side, h] = col_vals(4, side, h).astype(BF16)
+        lax.fori_loop(1, HE - 1, plain_row, 0)
+        for_dirs(lambda d: halo_copy(4, d, row_src), "recv", ROW_DIRS)
+        halo_rows(4)
+        for h in (0, HE - 1):
+            plain_row(h, 0)
+        for_dirs(lambda d: halo_copy(4, d, row_src), "recv", COL_DIRS)
+        lax.fori_loop(0, HE, plain_edges, 0)
         for_dirs(lambda d: halo_copy(4, d, row_src), "send")
         for n in range(4):
             for j in range(1, n_dev):
@@ -417,21 +438,7 @@
     main()
 
 
-def up_kernel(xe, ce, wu, ub, out, a_ref, sv, o32, part, ob, o_sem):
-    def row(h, c):
-        for side in PAIR:
-            v = ce[side, h].astype(F32)
-            for half in PAIR:
-                sv[half, pl.ds(7 + side * 25, T, stride=SW_), :] = v[0:T, half * LN:half * LN + LN]
-        for t in range(T):
-            v = xe[h, t].astype(F32)
-            for half in PAIR:
-                sv[half, pl.ds(t * SW_ + 8, W), :] = v[:, half * LN:half * LN + LN]
-        write_operand(a_ref, sv, h)
-        return c
-
-    lax.fori_loop(0, HE, row, 0)
-
+def up_kernel(a_ref, wu, ub, out, o32, part, ob, o_sem):
     def out_copy(q, a, hp):
         return pltpu.make_async_copy(ob.at[hp, q, a], out.at[:, 2 * (q * 3 + hp) + a], o_sem.at[hp, q, a])
 
@@ -516,11 +523,11 @@
         lat = latent[0].transpose(1, 2, 0, 3)
         cw = conv_weight.transpose(0, 1, 4, 5, 6, 2, 3).reshape(2, 2, 27, C, C)
         uw = up_weight.transpose(2, 3, 0, 1)
-        xe, ce = pl.pallas_call(
+        aup = pl.pallas_call(
             functools.partial(stage_kernel, n_sh, n_sw),
-            out_shape=(jax.ShapeDtypeStruct((HE, T, W, C), BF16), jax.ShapeDtypeStruct((2, HE, 16, C), BF16)),
+            out_shape=jax.ShapeDtypeStruct((3, HE, AR, C), BF16),
             in_specs=[hbm] * 10,
-            out_specs=(vmem, vmem),
+            out_specs=vmem,
             scratch_shapes=[
                 pltpu.VMEM((4, 27, C, C), BF16),
                 pltpu.VMEM((3, HE, AR, C), BF16),
@@ -538,33 +545,31 @@
                 pltpu.VMEM((2, T, W, C), BF16),
                 pltpu.VMEM((2, H, 16, C), BF16),
                 pltpu.VMEM((2, H * 16, 128), BF16),
-                pltpu.VMEM((2, T * SW_, 128), F32),
-                pltpu.VMEM((128, 2 * C), BF16),
-                pltpu.VMEM((4, 8, 128), F32),
-                pltpu.VMEM((4, n_dev, 8, 128), F32),
+                pltpu.VMEM((HE, 2, T * SW_, LN), F32),
+                pltpu.VMEM((LN, 2 * C), BF16),
+                pltpu.VMEM((4, 1, LN), F32),
+                pltpu.VMEM((4, n_dev, 1, LN), F32),
                 pltpu.VMEM((3, 8, C), F32),
                 vec, vec, mat, vec, mat, vec, vec,
                 dma((9,)), dma((4,)), dma((5, 8)), dma((5, 8)), dma((8,)), dma((8,)), dma((4, n_dev)), dma((4, n_dev)),
             ],
-            compiler_params=pltpu.CompilerParams(collective_id=0, has_side_effects=True, vmem_limit_bytes=40 << 20),
+            compiler_params=pltpu.CompilerParams(collective_id=0, has_side_effects=True, vmem_limit_bytes=42 << 20),
             name="stages",
         )(*[pltpu.with_memory_space_constraint(v, pltpu.HBM) for v in (feat, lat, gn_gain, gn_bias, zy_weight, zy_bias, zb_weight, zb_bias, cw, conv_bias)])
         out = pl.pallas_call(
             up_kernel,
             out_shape=jax.ShapeDtypeStruct((T, 2 * H, 2 * W, C), BF16),
-            in_specs=[vmem] * 4,
+            in_specs=[vmem] * 3,
             out_specs=hbm,
             scratch_shapes=[
-                pltpu.VMEM((3, HE, AR, C), BF16),
-                pltpu.VMEM((2, T * SW_, 128), F32),
-                pltpu.VMEM((2, 2, T * 2 * W, 128), F32),
+                pltpu.VMEM((2, 2, T * 2 * W, LN), F32),
                 pltpu.VMEM((2, 4, FR, C), F32),
                 pltpu.VMEM((3, 2, 2, T, 2 * W, C), BF16),
                 dma((3, 2, 2)),
             ],
-            compiler_params=pltpu.CompilerParams(vmem_limit_bytes=40 << 20),
+            compiler_params=pltpu.CompilerParams(vmem_limit_bytes=24 << 20),
             name="upsample",
-        )(xe, ce, uw, up_bias.reshape(1, C))
+        )(aup, uw, up_bias.reshape(1, C))
         return out.transpose(3, 0, 1, 2)[None]
 
     data_spec = P("dp", None, None, "sh", "sw")

time: 71.5 us -> 69.5 us (0.972)
  Pallas kernels: 71.2 us -> 69.2 us
    pallas_call x1, Pallas kernels: 8.98 us -> 7.98 us  [local_step(): pl.pallas_call(up_kernel, out_shape=jax.ShapeDtypeStruct((T, 2 * H, 2 * W...]
    pallas_call x1, Pallas kernels: 62.2 us -> 61.2 us  [local_step(): pl.pallas_call(functools.partial(stage_kernel, n_sh, n_sw), out_shape=jax...]
where the time goes in v3:
time: 69.5 us; the launch traced here: 69.4 us
  Pallas kernels  69.2 us (100%)
    pallas_call x1, Pallas kernels, local_step(): pl.pallas_call(functools.partial(stage_kernel, n_sh, n_sw), out_shape=jax...  61.2 us
    pallas_call x1, Pallas kernels, local_step(): pl.pallas_call(up_kernel, out_shape=jax.ShapeDtypeStruct((T, 2 * H, 2 * W...  7.98 us

profile of v3, /device:TPU:0, one launch (start us, length us, event | category | flops | bytes accessed | tf_op | source)
XLA Modules:
  0.0 69.4 jit_solution(7697381429187061432)
XLA Ops:
  0.0 0.0 copy-start
  0.0 0.0 copy-start.1
  0.0 61.2 %stages.1.a_ref = bf16[3,8,352,256]{3,2,1,0:T(8,128)(2,1)S(1)} custom-call(bf16[12,6,24,256]{3,2,1,0:T(8,128)(2,1)} %bitcast.17, bf16[12,6,16,24]{3,2,1,0:T(8,128)(2,1)} %bitcast.18, f32[2,2,256]{2,1,0:T(2,128)} %gain_in.1, f32[2,2,256]{2,1,0:T(2,128)} %gbias_in.1, bf16[2,2,16,256]{3,2,1,0:T(8,128)(2,1)} %zyw_in.1, f32[2,2,256]{2,1,0:T(2,128)} %zyb_in.1, ...), custom_call_target="tpu_custom_call" | custom-call | tf_op jit(solution)/shard_map/stages/pallas_call | solution.py:526
  61.2 0.0 copy-done
  61.2 0.0 copy-done.1
  61.2 8.0 %upsample.1 = bf16[12,12,48,256]{3,2,1,0:T(8,128)(2,1)} custom-call(bf16[3,8,352,256]{3,2,1,0:T(8,128)(2,1)S(1)} %stages.1.a_ref, bf16[3,3,256,256]{3,2,1,0:T(8,128)(2,1)S(1)} %bitcast.14, f32[1,256]{1,0:T(1,128)S(1)} %bitcast.15), custom_call_target="tpu_custom_call" | custom-call | tf_op jit(solution)/shard_map/upsample/pallas_call | solution.py:559
Async XLA Ops:
  0.0 61.2 %copy-start = (bf16[256,256,3,3]{1,0,3,2:T(8,128)(2,1)S(1)}, bf16[256,256,3,3]{1,0,3,2:T(8,128)(2,1)}, u32[]{:S(2)}) copy-start(bf16[256,256,3,3]{1,0,3,2:T(8,128)(2,1)} %param.22) | copy-start | bytes 3538948
  0.0 61.2 %copy-start.1 = (f32[256]{0:T(256)S(1)}, f32[256]{0:T(256)}, u32[]{:S(2)}) copy-start(f32[256]{0:T(256)} %param.23) | copy-start | bytes 3076

commit v4 on v3

--- a/solution.py
+++ b/solution.py
@@ -28,6 +28,7 @@
 LN = 128
 PAIR, TRIO = range(2), range(3)
 GAPS = (1, 2, 4)
+NTAP, EARLY = 27, 6
 TR, SUB = 16, 8
 
 
@@ -311,8 +312,8 @@
 
         def col_vals(e, side, h):
             cond = has["l"] if side == 0 else has["r"]
-            cond = jnp.logical_and(cond, jnp.logical_or(h > 0, has["u"]))
-            cond = jnp.logical_and(cond, jnp.logical_or(h < HE - 1, has["d"]))
+            cond = jnp.logical_and(cond, jnp.logical_or(jnp.int32(h) > 0, has["u"]))
+            cond = jnp.logical_and(cond, jnp.logical_or(jnp.int32(h) < HE - 1, has["d"]))
             return jnp.where(cond, ce[e, side, h].astype(F32), 0.0)
 
         def put_column(h, side, v):
@@ -322,20 +323,16 @@
         def own_rows(h, t, half):
             return rx[half, pl.ds(pl.multiple_of(h * FR, SUB) + t * W, W), :]
 
-        def activate_rows(n):
-            def row(h, c):
-                for side in PAIR:
-                    at = pl.ds(pl.multiple_of(side * LN + h * TR, TR), TR)
-                    put_column(h, side, activate(col_vals(n, side, h), yv[HE, at, :], bv[HE, at, :]))
-                for t in range(T):
-                    x = jnp.concatenate([own_rows(h, t, half) for half in PAIR], axis=1)
-                    v = activate(x, yv[h, pl.ds(t * W, W), :], bv[h, pl.ds(t * W, W), :])
-                    for half in PAIR:
-                        sv[h, half, pl.ds(t * SW_ + 8, W), :] = v[:, half * LN:half * LN + LN]
-                write_operand(a_ref, sv, h)
-                return c
-
-            lax.fori_loop(0, HE, row, 0)
+        def activate_row(n, h):
+            for side in PAIR:
+                at = pl.ds(pl.multiple_of(side * LN + h * TR, TR), TR)
+                put_column(h, side, activate(col_vals(n, side, h), yv[HE, at, :], bv[HE, at, :]))
+            for t in range(T):
+                x = jnp.concatenate([own_rows(h, t, half) for half in PAIR], axis=1)
+                v = activate(x, yv[h, pl.ds(t * W, W), :], bv[h, pl.ds(t * W, W), :])
+                for half in PAIR:
+                    sv[h, half, pl.ds(t * SW_ + 8, W), :] = v[:, half * LN:half * LN + LN]
+            write_operand(a_ref, sv, h)
 
         def plain_row(h, c):
             for t in range(T):
@@ -350,23 +347,23 @@
             write_operand(aup, sv, h, (0,), (2,))
             return c
 
-        def conv(n, rows, steps):
+        def conv(n, rows, taps):
             def lhs(h, part, tap):
                 kt, kh, kw = tap // 9, tap // 3 % 3, tap % 3
                 return a_ref[kw, h + kh, pl.ds(kt * 16 + (ABASE if part else 0), NB if part else NA), :]
 
-            for i in steps:
-                rhs = jnp.concatenate([wv[n, i * 3 + kw] for kw in TRIO], axis=1)
-                for h in rows:
-                    cols = [jnp.concatenate([lhs(h, part, i * 3 + kw) for part in PAIR], axis=0) for kw in TRIO]
-                    v = lax.dot_general(jnp.concatenate(cols, axis=1), rhs, CONTRACT_LAST, preferred_element_type=F32)
-                    if i == 0:
-                        cv[h] = v
-                    else:
-                        cv[h] += v
+            for h in rows:
+                rhs = jnp.concatenate([wv[n, i] for i in taps], axis=1)
+                cols = [jnp.concatenate([lhs(h, part, i) for part in PAIR], axis=0) for i in taps]
+                v = lax.dot_general(jnp.concatenate(cols, axis=1), rhs, CONTRACT_LAST, preferred_element_type=F32)
+                if taps[0] == 0:
+                    cv[h] = v
+                else:
+                    cv[h] += v
 
         def finish(b, s, rows, sums):
             bias = chan(cb, b, s)
+            second = s == 1
             pivot, s1, s2 = sums
             for h in rows:
                 for part in PAIR:
@@ -379,9 +376,9 @@
                             t, w0 = (i // 2) + (i % 2) * T2, 16
                         blk = v[i * nblk:(i + 1) * nblk]
                         r0 = t * W + w0
-                        if s == 1:
-                            blk = (blk + xres[h, pl.ds(r0, nblk), :]).astype(BF16).astype(F32)
-                            xres[h, pl.ds(r0, nblk), :] = blk
+                        res = xres[h, pl.ds(r0, nblk), :]
+                        blk = (blk + jnp.where(second, res, 0.0)).astype(BF16).astype(F32)
+                        xres[h, pl.ds(r0, nblk), :] = jnp.where(second, blk, res)
                         for half in PAIR:
                             rx[half, pl.ds((h + 1) * FR + r0, nblk), :] = blk[:, half * LN:half * LN + LN]
                         if h in (0, H - 1):
@@ -394,34 +391,38 @@
                             s2 = s2 + d * d
             return pivot, s1, s2
 
-        def block(b, carry):
-            for s in PAIR:
-                n = b * 2 + s
-                latent_maps(b, s)
-                for_dirs(lambda d: halo_copy(n, d, row_src), "recv")
-                halo_rows(n)
-                recv_stats(n, b, s)
-                activate_rows(n)
-                ld_weight(n, b, s).wait()
-                for_dirs(lambda d: halo_copy(n, d, row_src), "send")
-                conv(n, EDGE, range(9))
-                sums = finish(b, s, EDGE, (None, zero8, zero8))
-                fill_columns(EDGE)
-                conv(n, INNER, PAIR)
-                for_dirs(lambda d: halo_copy(n + 1, d, row_src), "start", ROW_DIRS)
-                conv(n, INNER, range(2, 9))
-                pivot, s1, s2 = finish(b, s, INNER, sums)
-                if s == 0:
-                    send_stats(n + 1, pivot, s1, s2)
-                else:
-                    @pl.when(b == 0)
-                    def _():
-                        send_stats(n + 1, pivot, s1, s2)
-                fill_columns(INNER)
-                for_dirs(lambda d: halo_copy(n + 1, d, row_src), "start", COL_DIRS)
+        def stage(n, carry):
+            b, s = n // 2, lax.rem(n, 2)
+            latent_maps(b, s)
+            for_dirs(lambda d: halo_copy(n, d, row_src), "recv")
+            halo_rows(n)
+            recv_stats(n, b, s)
+            lax.fori_loop(0, 3, lambda h, c: (activate_row(n, h), c)[1], 0)
+            ld_weight(n, b, s).wait()
+            for_dirs(lambda d: halo_copy(n, d, row_src), "send")
+            sums = (None, zero8, zero8)
+            for h, ahead in zip(EDGE, ((HE - 3, HE - 2, HE - 1), (3, 4))):
+                conv(n, (h,), range(NTAP))
+                for k in ahead:
+                    activate_row(n, k)
+                sums = finish(b, s, (h,), sums)
+            fill_columns(EDGE)
+            conv(n, INNER, range(EARLY))
+            for_dirs(lambda d: halo_copy(n + 1, d, row_src), "start", ROW_DIRS)
+            for h in INNER:
+                conv(n, (h,), range(EARLY, NTAP))
+                sums = finish(b, s, (h,), sums)
+            pivot, s1, s2 = sums
+
+            @pl.when(n < 3)
+            def _():
+                send_stats(n + 1, pivot, s1, s2)
+
+            fill_columns(INNER)
+            for_dirs(lambda d: halo_copy(n + 1, d, row_src), "start", COL_DIRS)
             return carry
 
-        lax.fori_loop(0, 2, block, 0)
+        lax.fori_loop(0, 4, stage, 0)
 
         lax.fori_loop(1, HE - 1, plain_row, 0)
         for_dirs(lambda d: halo_copy(4, d, row_src), "recv", ROW_DIRS)

time: 69.5 us -> 67.8 us (0.976)
  Pallas kernels: 69.2 us -> 67.5 us
    pallas_call x1, Pallas kernels: 61.2 us -> 59.5 us  [local_step(): pl.pallas_call(functools.partial(stage_kernel, n_sh, n_sw), out_shape=jax...]
where the time goes in v4:
time: 67.8 us; the launch traced here: 67.7 us
  Pallas kernels  67.5 us (100%)
    pallas_call x1, Pallas kernels, local_step(): pl.pallas_call(functools.partial(stage_kernel, n_sh, n_sw), out_shape=jax...  59.5 us
    pallas_call x1, Pallas kernels, local_step(): pl.pallas_call(up_kernel, out_shape=jax.ShapeDtypeStruct((T, 2 * H, 2 * W...  7.97 us

profile of v4, /device:TPU:0, one launch (start us, length us, event | category | flops | bytes accessed | tf_op | source)
XLA Modules:
  0.0 67.7 jit_solution(12632220842228980770)
XLA Ops:
  0.0 0.0 copy-start
  0.0 0.0 copy-start.1
  0.0 59.5 %stages.1.a_ref = bf16[3,8,352,256]{3,2,1,0:T(8,128)(2,1)S(1)} custom-call(bf16[12,6,24,256]{3,2,1,0:T(8,128)(2,1)} %bitcast.17, bf16[12,6,16,24]{3,2,1,0:T(8,128)(2,1)} %bitcast.18, f32[2,2,256]{2,1,0:T(2,128)} %gain_in.1, f32[2,2,256]{2,1,0:T(2,128)} %gbias_in.1, bf16[2,2,16,256]{3,2,1,0:T(8,128)(2,1)} %zyw_in.1, f32[2,2,256]{2,1,0:T(2,128)} %zyb_in.1, ...), custom_call_target="tpu_custom_call" | custom-call | tf_op jit(solution)/shard_map/stages/pallas_call | solution.py:527
  59.5 0.0 copy-done
  59.5 0.0 copy-done.1
  59.6 8.0 %upsample.1 = bf16[12,12,48,256]{3,2,1,0:T(8,128)(2,1)} custom-call(bf16[3,8,352,256]{3,2,1,0:T(8,128)(2,1)S(1)} %stages.1.a_ref, bf16[3,3,256,256]{3,2,1,0:T(8,128)(2,1)S(1)} %bitcast.14, f32[1,256]{1,0:T(1,128)S(1)} %bitcast.15), custom_call_target="tpu_custom_call" | custom-call | tf_op jit(solution)/shard_map/upsample/pallas_call | solution.py:560
Async XLA Ops:
  0.0 59.5 %copy-start = (bf16[256,256,3,3]{1,0,3,2:T(8,128)(2,1)S(1)}, bf16[256,256,3,3]{1,0,3,2:T(8,128)(2,1)}, u32[]{:S(2)}) copy-start(bf16[256,256,3,3]{1,0,3,2:T(8,128)(2,1)} %param.22) | copy-start | bytes 3538948
  0.0 59.5 %copy-start.1 = (f32[256]{0:T(256)S(1)}, f32[256]{0:T(256)}, u32[]{:S(2)}) copy-start(f32[256]{0:T(256)} %param.23) | copy-start | bytes 3076

commit v5 on v4

--- a/solution.py
+++ b/solution.py
@@ -28,7 +28,8 @@
 LN = 128
 PAIR, TRIO = range(2), range(3)
 GAPS = (1, 2, 4)
-NTAP, EARLY = 27, 6
+TAPS = [kt * 9 + kh * 3 + kw for kh in TRIO for kt in TRIO for kw in TRIO]
+EARLY = 6
 TR, SUB = 16, 8
 
 
@@ -397,20 +398,21 @@
             for_dirs(lambda d: halo_copy(n, d, row_src), "recv")
             halo_rows(n)
             recv_stats(n, b, s)
-            lax.fori_loop(0, 3, lambda h, c: (activate_row(n, h), c)[1], 0)
             ld_weight(n, b, s).wait()
             for_dirs(lambda d: halo_copy(n, d, row_src), "send")
+            for h in TRIO:
+                activate_row(n, h)
             sums = (None, zero8, zero8)
             for h, ahead in zip(EDGE, ((HE - 3, HE - 2, HE - 1), (3, 4))):
-                conv(n, (h,), range(NTAP))
+                conv(n, (h,), TAPS)
                 for k in ahead:
                     activate_row(n, k)
                 sums = finish(b, s, (h,), sums)
             fill_columns(EDGE)
-            conv(n, INNER, range(EARLY))
+            conv(n, INNER, TAPS[:EARLY])
             for_dirs(lambda d: halo_copy(n + 1, d, row_src), "start", ROW_DIRS)
             for h in INNER:
-                conv(n, (h,), range(EARLY, NTAP))
+                conv(n, (h,), TAPS[EARLY:])
                 sums = finish(b, s, (h,), sums)
             pivot, s1, s2 = sums
 

time: 67.8 us -> 67.1 us (0.990)
  Pallas kernels: 67.5 us -> 66.8 us
    pallas_call x1, Pallas kernels: 59.5 us -> 58.8 us  [local_step(): pl.pallas_call(functools.partial(stage_kernel, n_sh, n_sw), out_shape=jax...]
where the time goes in v5:
time: 67.1 us; the launch traced here: 67 us
  Pallas kernels  66.8 us (100%)
    pallas_call x1, Pallas kernels, local_step(): pl.pallas_call(functools.partial(stage_kernel, n_sh, n_sw), out_shape=jax...  58.8 us
    pallas_call x1, Pallas kernels, local_step(): pl.pallas_call(up_kernel, out_shape=jax.ShapeDtypeStruct((T, 2 * H, 2 * W...  7.99 us

profile of v5, /device:TPU:0, one launch (start us, length us, event | category | flops | bytes accessed | tf_op | source)
XLA Modules:
  0.0 67.0 jit_solution(5584919364806967704)
XLA Ops:
  0.0 0.0 copy-start
  0.0 0.0 copy-start.1
  0.0 58.8 %stages.1.a_ref = bf16[3,8,352,256]{3,2,1,0:T(8,128)(2,1)S(1)} custom-call(bf16[12,6,24,256]{3,2,1,0:T(8,128)(2,1)} %bitcast.17, bf16[12,6,16,24]{3,2,1,0:T(8,128)(2,1)} %bitcast.18, f32[2,2,256]{2,1,0:T(2,128)} %gain_in.1, f32[2,2,256]{2,1,0:T(2,128)} %gbias_in.1, bf16[2,2,16,256]{3,2,1,0:T(8,128)(2,1)} %zyw_in.1, f32[2,2,256]{2,1,0:T(2,128)} %zyb_in.1, ...), custom_call_target="tpu_custom_call" | custom-call | tf_op jit(solution)/shard_map/stages/pallas_call | solution.py:529
  58.8 0.0 copy-done
  58.8 0.0 copy-done.1
  58.8 8.0 %upsample.1 = bf16[12,12,48,256]{3,2,1,0:T(8,128)(2,1)} custom-call(bf16[3,8,352,256]{3,2,1,0:T(8,128)(2,1)S(1)} %stages.1.a_ref, bf16[3,3,256,256]{3,2,1,0:T(8,128)(2,1)S(1)} %bitcast.14, f32[1,256]{1,0:T(1,128)S(1)} %bitcast.15), custom_call_target="tpu_custom_call" | custom-call | tf_op jit(solution)/shard_map/upsample/pallas_call | solution.py:562
Async XLA Ops:
  0.0 58.8 %copy-start = (bf16[256,256,3,3]{1,0,3,2:T(8,128)(2,1)S(1)}, bf16[256,256,3,3]{1,0,3,2:T(8,128)(2,1)}, u32[]{:S(2)}) copy-start(bf16[256,256,3,3]{1,0,3,2:T(8,128)(2,1)} %param.22) | copy-start | bytes 3538948
  0.0 58.8 %copy-start.1 = (f32[256]{0:T(256)S(1)}, f32[256]{0:T(256)}, u32[]{:S(2)}) copy-start(f32[256]{0:T(256)} %param.23) | copy-start | bytes 3076

commit v6 on v5

--- a/solution.py
+++ b/solution.py
@@ -29,7 +29,7 @@
 PAIR, TRIO = range(2), range(3)
 GAPS = (1, 2, 4)
 TAPS = [kt * 9 + kh * 3 + kw for kh in TRIO for kt in TRIO for kw in TRIO]
-EARLY = 6
+EARLY = 9
 TR, SUB = 16, 8
 
 

time: 67.1 us -> 67 us (level)
  no operation moved by 1% of the time
where the time goes in v6:
time: 67 us; the launch traced here: 66.8 us
  Pallas kernels  66.7 us (100%)
    pallas_call x1, Pallas kernels, local_step(): pl.pallas_call(functools.partial(stage_kernel, n_sh, n_sw), out_shape=jax...  58.7 us
    pallas_call x1, Pallas kernels, local_step(): pl.pallas_call(up_kernel, out_shape=jax.ShapeDtypeStruct((T, 2 * H, 2 * W...  7.98 us

profile of v6, /device:TPU:0, one launch (start us, length us, event | category | flops | bytes accessed | tf_op | source)
XLA Modules:
  0.0 66.8 jit_solution(7329744723155920657)
XLA Ops:
  0.0 0.0 copy-start
  0.0 0.0 copy-start.1
  0.0 58.7 %stages.1.a_ref = bf16[3,8,352,256]{3,2,1,0:T(8,128)(2,1)S(1)} custom-call(bf16[12,6,24,256]{3,2,1,0:T(8,128)(2,1)} %bitcast.17, bf16[12,6,16,24]{3,2,1,0:T(8,128)(2,1)} %bitcast.18, f32[2,2,256]{2,1,0:T(2,128)} %gain_in.1, f32[2,2,256]{2,1,0:T(2,128)} %gbias_in.1, bf16[2,2,16,256]{3,2,1,0:T(8,128)(2,1)} %zyw_in.1, f32[2,2,256]{2,1,0:T(2,128)} %zyb_in.1, ...), custom_call_target="tpu_custom_call" | custom-call | tf_op jit(solution)/shard_map/stages/pallas_call | solution.py:529
  58.7 0.0 copy-done
  58.7 0.0 copy-done.1
  58.7 8.0 %upsample.1 = bf16[12,12,48,256]{3,2,1,0:T(8,128)(2,1)} custom-call(bf16[3,8,352,256]{3,2,1,0:T(8,128)(2,1)S(1)} %stages.1.a_ref, bf16[3,3,256,256]{3,2,1,0:T(8,128)(2,1)S(1)} %bitcast.14, f32[1,256]{1,0:T(1,128)S(1)} %bitcast.15), custom_call_target="tpu_custom_call" | custom-call | tf_op jit(solution)/shard_map/upsample/pallas_call | solution.py:562
Async XLA Ops:
  0.0 58.7 %copy-start = (bf16[256,256,3,3]{1,0,3,2:T(8,128)(2,1)S(1)}, bf16[256,256,3,3]{1,0,3,2:T(8,128)(2,1)}, u32[]{:S(2)}) copy-start(bf16[256,256,3,3]{1,0,3,2:T(8,128)(2,1)} %param.22) | copy-start | bytes 3538948
  0.0 58.7 %copy-start.1 = (f32[256]{0:T(256)S(1)}, f32[256]{0:T(256)}, u32[]{:S(2)}) copy-start(f32[256]{0:T(256)} %param.23) | copy-start | bytes 3076
